TPU v7x, 8 devices: a whole 2x2x1 slice. The times are simulated.
8 devices in a mesh: model: 2 (over z, y), data: 4 (over x, core).
Axes of the slice: x: 2, y: 2, z: 1, core: 2. Of those that a mesh axis runs over, the one named last changes fastest.
Arguments:
- h_a: bfloat16 [16384, 2048], P('data')
- h_b: bfloat16 [16384, 2048], P('data')
- w_one: bfloat16 [2048, 2048], P(None, 'model')
- w_two: bfloat16 [2048, 2048], P('model')
- w_three: bfloat16 [2048, 2048], P(None, 'model')
- g_one: float32 [2048], P('model')
- b_one: float32 [2048], P('model')
- g_two: float32 [2048], replicated
- b_two: float32 [2048], replicated
- lam_off: float32 [1], replicated
Outputs:
- output 1: float32 [1], replicated
- output 2: float32 [2048, 2048], P(None, 'model')
- output 3: float32 [2048, 2048], P('model')
- output 4: float32 [2048, 2048], P(None, 'model')
- output 5: float32 [2048], P('model')
- output 6: float32 [2048], P('model')
- output 7: float32 [2048], replicated
- output 8: float32 [2048], replicated
All inputs are finite; a program needn't handle non-finite values.
Results may differ from a plain program's by a relative error of at most 0.001.
Values are sent between devices in bfloat16 or wider.
A program may use at most 1 GiB of HBM per device.

v0:
```python
import functools

import jax
import jax.numpy as jnp
from jax import lax
from jax.experimental import pallas as pl
from jax.experimental.pallas import tpu as pltpu
from jax.sharding import PartitionSpec as P

BN_EPS = 1e-5
F32 = jnp.float32
BF16 = jnp.bfloat16
PIECE = 64
LANES = 256
SUBLANES = 8
TM = 512
MAX_VMEM = 67043328
ANY = pl.BlockSpec(memory_space=pl.ANY)
VMEM = pl.BlockSpec(memory_space=pltpu.VMEM)
DMA = pltpu.SemaphoreType.DMA
TWO_DMA = DMA((2,))
BOTH = (0, 1)
PEERS = [(ky, kx, kc) for ky in BOTH for kx in BOTH for kc in BOTH][1:]
C_PEER, X_PEER, Y_PEER = PEERS[0], PEERS[1], PEERS[3]
N_DEV = len(PEERS) + 1


def mm(left, right):
    return jnp.dot(left, right, preferred_element_type=F32)


def mm_bt(left, right):
    return lax.dot_general(left, right, (((1,), (1,)), ((), ())), preferred_element_type=F32)


def mm_at(left, right):
    return lax.dot_general(left, right, (((0,), (0,)), ((), ())), preferred_element_type=F32)


def other(p):
    return 1 - p


def odd(i):
    return lax.rem(i, 2)


def split(i):
    return lax.div(i, 2), odd(i)


def loop(n, body, start=0):
    def one(i, carry):
        body(i)
        return carry

    lax.fori_loop(start, n, one, 0)


def whole(*shape):
    return pl.BlockSpec(shape, lambda *_: (0,) * len(shape))


def at(i, n):
    return pl.ds(pl.multiple_of(i * n, n), n)


def sds(shape, dtype):
    return jax.ShapeDtypeStruct(shape, dtype)


def mean_inv(sums, total):
    mean = sums[:1] / total
    var = sums[1:2] / total - mean * mean
    return mean, lax.rsqrt(var + BN_EPS)


def fold(v):
    return jnp.sum(v.reshape(-1, SUBLANES, v.shape[1]), axis=0)


def runs(n, size):
    return [pl.ds(r, size) for r in range(0, n, size)]


def two_sums(pairs):
    one = two = 0.0
    for a, b in pairs:
        one, two = one + fold(a), two + fold(b)
    return jnp.concatenate([jnp.sum(t, axis=0, keepdims=True) for t in (one, two)], axis=0)


def moments(ref, cols):
    pieces = (ref[r, cols] for r in runs(ref.shape[0], PIECE))
    return two_sums((u, u * u) for u in pieces)


def coords():
    y, d = lax.axis_index('model'), lax.axis_index('data')
    return y, lax.div(d, 2), odd(d)


def flip(here, which):
    return tuple(other(p) if f else p for p, f in zip(here, which))


def flat(here):
    y, x, c = here
    return 4 * y + 2 * x + c


def device(here):
    y, x, c = here
    return (y, 2 * x + c)


def remote(src, dst, send_sem, recv_sem, there):
    return pltpu.make_async_remote_copy(
        src_ref=src, dst_ref=dst, send_sem=send_sem, recv_sem=recv_sem, device_id=device(there),
        device_id_type=pl.DeviceIdType.MESH)


def arrive():
    here = coords()
    for k in PEERS:
        pl.semaphore_signal(pltpu.get_barrier_semaphore(), inc=1, device_id=device(flip(here, k)),
                            device_id_type=pl.DeviceIdType.MESH)


def all_arrived():
    pl.semaphore_wait(pltpu.get_barrier_semaphore(), len(PEERS))


class Share:
    def __init__(self, acc, got, send_sem, recv_sem):
        self.acc, self.got, self.send_sem, self.recv_sem = acc, got, send_sem, recv_sem

    @staticmethod
    def scratch(n, *shape):
        return [pltpu.VMEM((n, *shape), F32), pltpu.VMEM((n, N_DEV, *shape), F32), DMA((n,)), DMA((n,))]

    def start(self, b):
        here = coords()
        me = flat(here)
        self.got[b, me] = self.acc[b]
        for which in PEERS:
            remote(self.acc.at[b], self.got.at[b, me], self.send_sem.at[b], self.recv_sem.at[b],
                   flip(here, which)).start()

    def total(self, b):
        all_of = self.got.at[b, pl.ds(0, len(PEERS))]
        copies = remote(all_of, all_of, self.send_sem.at[b], self.recv_sem.at[b], coords())
        copies.wait_send()
        copies.wait_recv()
        out = self.got[b, 0]
        for f in range(1, N_DEV):
            out += self.got[b, f]
        return out


class Gather:
    def __init__(self, own, dest, n, sems):
        self.own, self.dest, self.n = own, dest, n
        self.ys, self.yr, self.xs, self.xr, self.cs, self.cr = sems
        self.here = coords()
        _, x, c = self.here
        self.mine, self.across = 2 * x + c, 2 * (other(x)) + c
        self.core = (2 * x + other(c), 2 * (other(x)) + other(c))

    @staticmethod
    def scratch(n):
        return [DMA((n,))] * 4 + [DMA((2, n))] * 2

    def y(self, p):
        model = self.here[0]
        return remote(self.own(self.mine, p), self.dest(model, self.mine, p), self.ys.at[p], self.yr.at[p],
                      flip(self.here, Y_PEER))

    def moved(self, q, p, send_sem, recv_sem, which):
        ref = self.dest(1 - self.here[0], q, p)
        return remote(ref, ref, send_sem, recv_sem, flip(self.here, which))

    def x(self, p, q):
        return self.moved(q, p, self.xs.at[p], self.xr.at[p], X_PEER)

    def c(self, p, late, q):
        return self.moved(q, p, self.cs.at[late, p], self.cr.at[late, p], C_PEER)

    def start(self):
        for p in range(self.n):
            self.y(p).start()

    def pass_y(self, p):
        self.moved(self.mine, p, self.ys.at[p], self.yr.at[p], Y_PEER).wait_recv()
        self.x(p, self.mine).start()
        self.c(p, 0, self.mine).start()

    def pass_x(self, p):
        self.x(p, self.across).wait_recv()
        self.c(p, 1, self.across).start()

    def wait_core(self, late):
        for p in range(self.n):
            self.c(p, late, self.core[late]).wait_recv()

    def drain(self):
        for p in range(self.n):
            self.y(p).wait_send()
            self.x(p, self.mine).wait_send()
            self.c(p, 0, self.mine).wait_send()
            self.c(p, 1, self.across).wait_send()


def call(kernel, name, cid, grid, in_specs, out_specs, out_shape, scratch, flops, nbytes, args):
    return pl.pallas_call(
        kernel, name=name, grid=grid, in_specs=in_specs, out_specs=out_specs, out_shape=out_shape, scratch_shapes=scratch,
        compiler_params=pltpu.CompilerParams(vmem_limit_bytes=MAX_VMEM, collective_id=cid, has_side_effects=cid is not None),
        cost_estimate=pl.CostEstimate(flops=flops, bytes_accessed=nbytes, transcendentals=0))(*args)


def fwd_first(h_a, h_b, w_one, w_two, gb_own):
    depth, half = w_one.shape
    dim = 2 * half
    rows = h_a.shape[0] // 2
    tile, width, quarter = 2 * TM, half // 2, half // 4
    steps = rows // tile
    per_block = 2 * steps
    n, n2 = 4, 8

    def block(j):
        y, x, _ = coords()
        return jnp.where(j < 2, 2 * y + j, 2 * (other(y)) + jnp.where(j == 2, x, other(x)))

    def tile_of(j, i):
        return jnp.where(odd(j) == 0, i, per_block - 1 - i)

    def kernel(ha_ref, hb_ref, w_ref, w2_ref, gb_ref, u_ref, s_ref, gbo_ref, w2o_ref, ht_ref, w1, gbf, *sems):
        share, sems = Share(*sems[:4]), sems[4:]
        gs, gr, lsem = sems[:3]
        sems = sems[3:]
        j, i = pl.program_id(0), pl.program_id(1)
        step = j * per_block + i
        here = coords()
        y = here[0]
        one = Gather(lambda q, p: w_ref.at[at(p, depth // n), at(q, quarter)],
                     lambda m, q, p: w1.at[at(p, depth // n), at(m * 4 + q, quarter)], n, sems[:6])
        two = Gather(lambda q, p: w2_ref.at[at(q * n2 + p, quarter // n2)],
                     lambda m, q, p: w2o_ref.at[at(q * n2 + p, quarter // n2)], n2, sems[6:])

        def local(b):
            return pltpu.make_async_copy(w_ref.at[:, at(b, width)], w1.at[:, at(2 * y + b, width)], lsem.at[b])

        def bn_vectors(m):
            return remote(gb_ref, gbf.at[:, at(m, half)], gs, gr, flip(here, Y_PEER))

        def begin():
            arrive()
            local(0).start()
            local(1).start()
            all_arrived()
            one.start()
            two.start()
            bn_vectors(y).start()
            local(0).wait()

        def late_half():
            one.pass_x(0)
            one.pass_y(n - 1)
            one.wait_core(0)

        hooks = [(0, begin), (per_block, lambda: local(1).wait()), (2 * per_block, late_half)]
        hooks += [(2 * p + 3, functools.partial(one.pass_y, p)) for p in range(n - 1)]
        hooks += [(p + 2 * per_block, functools.partial(one.pass_x, p)) for p in range(1, n)]
        hooks += [(3 * per_block, lambda: one.wait_core(1))]
        hooks += [(p + 9, functools.partial(two.pass_y, p)) for p in range(n2 - 1)]
        hooks += [(13 + (p + 1) // 2, functools.partial(two.pass_x, p)) for p in range(n2 // 2)]
        for s, hook in hooks:
            pl.when(step == s)(hook)
        for b in range(3):
            pl.when(step == (b + 1) * per_block)(lambda b=b: share.start(block(b)))

        tile_at = tile_of(j, i)
        first_view = tile_at < steps
        cols = at(j, width)
        ht_ref[...] = lax.select(first_view, ha_ref[:, cols], hb_ref[:, cols]).T
        for r in runs(tile, TM):
            u_ref[r] = mm(lax.select(first_view, ha_ref[r], hb_ref[r]), w1[:, at(block(j), width)])
        sums = jnp.concatenate([moments(u_ref, cols) for cols in runs(width, LANES)], axis=1)
        v = tile_at // steps
        share.acc[block(j), v] = jnp.where(i % steps == 0, 0.0, share.acc[block(j), v]) + sums

        @pl.when(step == 4 * per_block - 1)
        def _():
            share.start(block(3))
            two.pass_y(n2 - 1)
            for p in range(n2 // 2, n2):
                two.pass_x(p)
            bn_vectors(other(y)).wait_recv()
            bn_vectors(y).wait_send()
            gbo_ref[...] = gbf[...]
            gbo_ref[:, at(y, half)] = gb_ref[...]
            for b in range(4):
                s_ref[:, :, b * width:(b + 1) * width] = share.total(b)
            one.drain()
            two.drain()
            two.wait_core(0)
            two.wait_core(1)

    return call(
        kernel, "fwd_first", 0, (4, per_block),
        [pl.BlockSpec((tile, depth), lambda j, i: (coords()[0] * steps + jnp.minimum(tile_of(j, i), steps - 1), 0)),
         pl.BlockSpec((tile, depth), lambda j, i: (coords()[0] * steps + jnp.maximum(tile_of(j, i) - steps, 0), 0)),
         ANY, ANY, whole(2, half)],
        [pl.BlockSpec((tile, width), lambda j, i: (tile_of(j, i), block(j))), whole(2, 2, dim),
         whole(2, dim), ANY, pl.BlockSpec((width, tile), lambda j, i: (j, tile_of(j, i)))],
        [sds((2 * rows, dim), F32), sds((2, 2, dim), F32), sds((2, dim), F32), sds((half, dim), BF16),
         sds((depth, 2 * rows), BF16)],
        [pltpu.VMEM((depth, dim), BF16), pltpu.VMEM((2, dim), F32)] + Share.scratch(4, 2, 2, width)
        + [DMA, DMA, TWO_DMA] + Gather.scratch(n) + Gather.scratch(n2),
        4 * rows * depth * dim, 2 * rows * (8 * depth + 4 * dim), (h_a, h_b, w_one, w_two, gb_own))


def fwd_next(u, sums, gb, w_own, w_other, by_rows, total, cid, w_next=None):
    all_rows, depth = u.shape
    dim = w_own.shape[1] if by_rows else 2 * w_own.shape[1]
    half = dim // 2
    quarter = half // 4
    steps = all_rows // 2 // TM
    last = 2 * steps - 1
    slab = dim // (2 * steps)
    n = 4

    def kernel(u_ref, s_ref, gb_ref, wo_ref, wt_ref, *refs):
        if w_next is not None:
            wn_ref, refs = refs[0], refs[1:]
        x_ref, o_ref, so_ref, wtr_ref, *refs = refs
        if w_next is not None:
            wno_ref, *refs = refs
        w, act, acc, got, ssem, rsem, lsem, *refs = refs
        share = Share(acc, got, ssem, rsem)
        i = pl.program_id(0)
        y = coords()[0]

        def local(ref, model, b):
            where = at(model, half)
            return pltpu.make_async_copy(ref, w.at[where] if by_rows else w.at[:, where], lsem.at[b])

        if w_next is not None:
            gather = Gather(lambda q, p: wn_ref.at[at(p, depth // n), at(q, quarter)],
                            lambda m, q, p: wno_ref.at[at(p, depth // n), at(q, quarter)], n, refs)

        @pl.when(i == 0)
        def _():
            arrive()
            acc[...] = jnp.zeros_like(acc)
            local(wo_ref, y, 0).start()
            local(wt_ref, other(y), 1).start()
            all_arrived()
            if w_next is not None:
                gather.start()
            local(wo_ref, y, 0).wait()
            local(wt_ref, other(y), 1).wait()

        if w_next is not None:
            for p in range(n):
                pl.when(i == p + 1)(lambda p=p: gather.pass_y(p))
                pl.when(i == p + 3)(lambda p=p: gather.pass_x(p))
        pl.when(i == steps)(lambda: share.start(0))

        mean, inv = mean_inv(s_ref[0], total)
        for k, cols in enumerate(runs(depth, LANES)):
            m, r, g, b = (t[:, k * LANES:(k + 1) * LANES] for t in (mean, inv, gb_ref[:1], gb_ref[1:]))
            for piece in runs(TM, PIECE):
                act[piece, cols] = jnp.maximum((u_ref[piece, cols] - m) * r * g + b, 0.0).astype(BF16)
        x_ref[...] = act[...].T
        wtr_ref[...] = w[:, at(i, slab)].T
        v = i // steps
        keep = jnp.where(i % steps == 0, 0.0, 1.0)
        for some in runs(dim, TM):
            o_ref[:, some] = mm(act[...], w[:, some])
            for cols in runs(TM, LANES):
                cols = pl.ds(some.start + cols.start, LANES)
                share.acc[v, :, cols] = keep * share.acc[v, :, cols] + moments(o_ref, cols)

        @pl.when(i == last)
        def _():
            share.start(1)
            for b in BOTH:
                so_ref[b] = share.total(b)
            if w_next is not None:
                gather.drain()
                gather.wait_core(0)
                gather.wait_core(1)

    more = w_next is not None
    return call(
        kernel, "fwd_next", cid, (2 * steps,),
        [pl.BlockSpec((TM, depth), lambda i: (i, 0)), pl.BlockSpec((1, 2, depth), lambda i: (i // steps, 0, 0)),
         whole(2, depth), ANY, ANY] + [ANY] * more,
        [pl.BlockSpec((depth, TM), lambda i: (0, i)), pl.BlockSpec((TM, dim), lambda i: (i, 0)),
         whole(2, 2, dim), pl.BlockSpec((slab, depth), lambda i: (i, 0))] + [ANY] * more,
        [sds((depth, all_rows), BF16), sds((all_rows, dim), F32), sds((2, 2, dim), F32), sds((dim, depth), BF16)]
        + ([sds(w_next.shape, BF16)] if more else []),
        [pltpu.VMEM((depth, dim), BF16), pltpu.VMEM((TM, depth), BF16)] + Share.scratch(2, 2, dim) + [TWO_DMA] + (Gather.scratch(n) if more else []),
        2 * all_rows * depth * dim, all_rows * (6 * depth + 4 * dim),
        (u, sums, gb, w_own, w_other) + ((w_next,) if more else ()))


def corr_grad(z, sums, lam, total):
    all_rows, dim = z.shape
    rows = all_rows // 2
    half = dim // 2
    quart = half // 2
    n_chunk = 8
    width = half // n_chunk
    pair = 2 * width
    mt = TM
    zt = TM // 2
    ahead = 3
    lead = 4
    z_steps = all_rows // zt
    m_steps = rows // mt
    scale = 1.0 / total

    def kernel(z_ref, s_ref, lam_ref, zho_ref, d_ref, so_ref, lo_ref, zh, da, ck, r1, r2, g, stage, dsend, drecv, acc, got, ssem, rsem, loss_acc, loss_got, lsem, lrsem, zs, zos,
               d1s, d1r, s1s, s1r, s2s, s2r, a2s, a2r, a1s, a1r, ads, adr, dbs, das):
        share = Share(acc, got, ssem, rsem)
        share_loss = Share(loss_acc, loss_got, lsem, lrsem)
        here = coords()
        y, x, c = here
        on_x = c == 0
        by_core = lambda one, two: tuple(jnp.where(on_x, a, b) for a, b in zip(one, two))
        first = by_core(flip(here, X_PEER), flip(here, Y_PEER))
        second = by_core(flip(here, Y_PEER), flip(here, X_PEER))
        cpeer = flip(here, C_PEER)
        bit1, bit2 = by_core((x, y), (y, x))
        arrive()
        acc[...] = jnp.zeros_like(acc)
        loss_acc[...] = jnp.zeros_like(loss_acc)

        def load(i, slot):
            return pltpu.make_async_copy(z_ref.at[at(i, zt)], ck.at[at(slot, zt)], zs.at[slot])

        def zh_out(i):
            v, r = lax.div(i, n_chunk // 2), lax.rem(i, n_chunk // 2)
            return pltpu.make_async_copy(zh.at[v, at(r, TM)], zho_ref.at[v, at(r, TM)], zos.at[i])

        z_slots = half // zt
        for i in range(ahead):
            load(i, i).start()

        def normalise(i):
            slot = lax.rem(i, z_slots)
            v, r = lax.div(i, z_steps // 2), lax.rem(i, z_steps // 2)
            pl.when(i + ahead < z_steps)(lambda: load(i + ahead, lax.rem(i + ahead, z_slots)).start())
            load(i, slot).wait()
            mean, inv = mean_inv(s_ref[v], total)
            for k, cols in enumerate(runs(dim, LANES)):
                m, s = (t[:, k * LANES:(k + 1) * LANES] for t in (mean, inv))
                for p in range(zt // PIECE):
                    zh[v, at(r * (zt // PIECE) + p, PIECE), cols] = (
                        (ck[at(slot * (zt // PIECE) + p, PIECE), cols] - m) * s).astype(BF16)
            da[at(i, rows // z_steps)] = jnp.zeros((rows // z_steps, dim), F32)

        loop(z_steps, normalise)
        all_arrived()

        def both(v, rows_at, t):
            return jnp.concatenate([zh[v, rows_at, at(b * n_chunk + t, width)] for b in BOTH], axis=1)

        group = lambda t, b: at(2 * t + b, width)

        def to_core(t):
            return remote(dsend.at[odd(t)], drecv.at[odd(t)], d1s.at[t], d1r.at[t], cpeer)

        def to_first(t):
            return remote(ck.at[:, group(t, other(bit1))], r1.at[t], s1s.at[t], s1r.at[t], first)

        def to_second(t):
            return remote(ck.at[at(other(bit2), quart), group(t, bit1)], r2.at[t], s2s.at[t], s2r.at[t], second)

        def g_second(t, b):
            block = g.at[t, at(2 * c + b, quart), at(bit1, width)]
            return remote(block, block, a2s.at[t], a2r.at[t], second)

        def g_first(t, b):
            block = g.at[t, at(c, half), at(b, width)]
            return remote(block, block, a1s.at[t], a1r.at[t], first)

        def g_core(t, core):
            block = g.at[t, at(core, half)]
            return remote(block, block, ads.at[t], adr.at[t], cpeer)

        def chip_sum(t):
            to_core(t).wait_recv()
            to_core(t).wait_send()
            ck[:, at(t, pair)] += drecv[odd(t)]
            pl.when(t < lead - 1)(lambda: to_first(t).start())

        def corr_part(t):
            zh_out(t).start()
            right = both(1, pl.ds(0, rows), t)
            dsend[odd(t)] = mm_at(zh[0, :, at(other(c), half)], right)
            ck[:, at(t, pair)] = mm_at(zh[0, :, at(c, half)], right)
            to_core(t).start()

        def db_out(t, m, slot, b):
            return pltpu.make_async_copy(
                stage.at[slot, :, at(b, width)], d_ref.at[1, at(m, mt), at(b * n_chunk + t, width)], dbs.at[slot, b])

        def da_out(m):
            return pltpu.make_async_copy(da.at[at(m, mt)], d_ref.at[0, at(m, mt)], das.at[m])

        def finish(m):
            def scaled(cols):
                for p in range(mt // PIECE):
                    some = at(m * (mt // PIECE) + p, PIECE)
                    d = da[some, cols] * scale
                    da[some, cols] = d
                    yield d, d * zh[0, some, cols].astype(F32)

            for cols in runs(dim, LANES):
                acc[0, :, cols] += two_sums(scaled(cols))
            da_out(m).start()

        def grads(t):
            def rows_of(m):
                slot = odd(m)

                @pl.when(t * m_steps + m >= 2)
                def _():
                    for b in BOTH:
                        db_out(t, m, slot, b).wait()

                own = both(1, at(m, mt), t)
                stage[slot] = mm(zh[0, at(m, mt)], g[t]) * scale
                sums = two_sums((stage[slot, r], stage[slot, r] * both(1, at(m * (mt // PIECE) + p, PIECE), t).astype(F32))
                                for p, r in enumerate(runs(mt, PIECE)))
                for b in BOTH:
                    acc[1, :, at(b * n_chunk + t, width)] += sums[:, b * width:(b + 1) * width]
                    db_out(t, m, slot, b).start()
                for cols in runs(dim, LANES):
                    da[at(m, mt), cols] += mm_bt(own, g[t, cols])
                pl.when(t == n_chunk - 1)(lambda: finish(m))

            loop(m_steps, rows_of)

        def at_first(t):
            to_first(t).wait_recv()
            ck[:, group(t, bit1)] += r1[t]
            to_second(t).start()

        def at_second(t):
            to_second(t).wait_recv()
            corr_mat = (ck[at(bit2, quart), group(t, bit1)] + r2[t]) * scale
            row_ids = (2 * c + bit2) * quart + lax.broadcasted_iota(jnp.int32, (quart, width), 0)
            col_ids = (bit1 * n_chunk + t) * width + lax.broadcasted_iota(jnp.int32, (quart, width), 1)
            is_diag = row_ids == col_ids
            lam_val = lam_ref[0]
            loss = jnp.where(is_diag, (1.0 - corr_mat) * (1.0 - corr_mat), lam_val * corr_mat * corr_mat)
            loss_acc[0] += jnp.sum(loss, axis=0, keepdims=True)
            pl.when(t == n_chunk - 1)(lambda: share_loss.start(0))
            grad = jnp.where(is_diag, -2.0 * (1.0 - corr_mat), 2.0 * lam_val * corr_mat).astype(BF16)
            g[t, at(2 * c + bit2, quart), at(bit1, width)] = grad
            g_second(t, bit2).start()

        def back_second(t):
            g_second(t, other(bit2)).wait_recv()
            g_first(t, bit1).start()
            pl.when(t + lead - 1 < n_chunk)(lambda: to_first(t + lead - 1).start())

        def back_first(t):
            g_first(t, other(bit1)).wait_recv()
            g_core(t, c).start()

        def back_core(t):
            g_core(t, other(c)).wait_recv()
            grads(t)

        def advance(tau):
            for lag, stage_fn in ((lead, at_first), (lead + 2, back_core), (lead + 1, back_first), (lead, at_second),
                                  (1, chip_sum), (0, corr_part), (lead, back_second)):
                t = tau - lag
                pl.when(jnp.logical_and(t >= 0, t < n_chunk))(lambda t=t, stage_fn=stage_fn: stage_fn(t))

        loop(n_chunk + lead + 2, advance)
        share.start(1)
        share.start(0)
        for t in range(n_chunk):
            for copy in (to_first(t), to_second(t), g_second(t, bit2), g_first(t, bit1), g_core(t, c)):
                copy.wait_send()
        for b in BOTH:
            so_ref[b] = share.total(b)
            for slot in BOTH:
                db_out(0, 0, slot, b).wait()
        lo_ref[...] = share_loss.total(0)
        for i in range(n_chunk):
            zh_out(i).wait()
        for m in range(m_steps):
            da_out(m).wait()

    return call(
        kernel, "corr_grad", 3, (), [ANY, VMEM, pl.BlockSpec(memory_space=pltpu.SMEM)], [ANY, ANY, VMEM, VMEM],
        [sds((2, rows, dim), BF16), sds((2, rows, dim), F32), sds((2, 2, dim), F32), sds((1, width), F32)],
        [pltpu.VMEM((2, rows, dim), BF16), pltpu.VMEM((rows, dim), F32), pltpu.VMEM((half, dim), F32),
         pltpu.VMEM((n_chunk, half, width), F32), pltpu.VMEM((n_chunk, quart, width), F32),
         pltpu.VMEM((n_chunk, dim, pair), BF16), pltpu.VMEM((2, mt, pair), F32)]
        + [pltpu.VMEM((2, half, pair), F32)] * 2 + Share.scratch(2, 2, dim) + Share.scratch(1, 1, width)
        + [DMA((half // zt,)), DMA((n_chunk,))] + [DMA((n_chunk,))] * 12 + [DMA((2, 2)), DMA((m_steps,))],
        all_rows * dim * dim * 3, all_rows * dim * 12, (z, sums, lam))


def backward(d_emb, zh, sz, s_emb, layers, x2_t, total):
    all_rows, dim = zh.shape
    rows, half = all_rows // 2, dim // 2
    width = 256
    slabs = dim // width
    items = 2 * slabs
    piece = width
    side = half // 2 // piece
    per_slab = half // piece
    n_layer = len(layers) + 1
    n_slab = n_layer * slabs
    per_layer = slabs * side
    n_chunk = n_layer * per_layer
    ahead = 3
    (u2, s2, gb2, w3_t, x1_t), (u1, s1, gb1, w2_t, h_t) = layers

    def kernel(d_ref, zh_ref, sz_ref, sd_ref, x2_ref, x1_ref, h_ref, u2_ref, u1_ref, w3_ref, w2_ref,
               s2_ref, s1_ref, gb2_ref, gb1_ref, dw3_ref, dw2_ref, dw1_ref, sum_ref, dy_ref, part_ref, ry_ref, rx_ref,
               dbuf, xbuf, d0, d1, wbuf, ubuf, dybuf, dyout, psend, pkeep, dr, ebuf, mbuf, fbuf, acc, got, ssem, rsem,
               us, ws, ds, dos, xl, ps, pr, pm, ys, yr, xs, xr, es, fs, fcs, fcr, credit):
        share = Share(acc, got, ssem, rsem)
        here = coords()
        y, x, c = here
        ypeer, xpeer, cpeer = flip(here, Y_PEER), flip(here, X_PEER), flip(here, C_PEER)
        arrive()

        def column(k, n):
            model = odd(n + jnp.where(k == 0, other(y), 0))
            return jnp.where(k == 1, n, model * (slabs // 2) + lax.div(n, 2))

        def turn(k):
            return jnp.where(k == 0, 0, other(y))

        def m_slot(j):
            return lax.rem(j, 4)

        def copy(src, dst, sem):
            return pltpu.make_async_copy(src, dst, sem)

        def sent_by(q):
            first = jnp.minimum(per_slab * lax.div(q, 4), per_layer)
            middle = jnp.clip(side * lax.div(q - 2 * items - 2, 2), 0, per_layer)
            last = jnp.clip(per_slab * lax.div(q - 4 * items - 2, 4), 0, per_layer)
            return first + middle + last

        def begun(q):
            return jnp.maximum(lax.div(q - 6, 2), 0)

        def to_core(s):
            return remote(psend.at[odd(s)], dr.at[odd(s)], ps.at[s], pr.at[s], cpeer)

        def keep_out(s):
            return copy(pkeep.at[odd(s)], part_ref.at[s], pm)

        def chip_sum(s):
            to_core(s).wait_recv()
            pkeep[odd(s)] += dr[odd(s)]

            @pl.when(s + 2 < n_slab)
            def _():
                pl.semaphore_signal(credit, inc=1, device_id=device(cpeer), device_id_type=pl.DeviceIdType.MESH)

            to_core(s).wait_send()
            keep_out(s).start()

        def home(j, own):
            k = lax.div(j, per_layer)
            i = lax.rem(j, per_layer)
            model = y if own else other(y)
            turned = other(turn(k)) if own else turn(k)
            s = jnp.where(k == 1, lax.div(i, side), 2 * lax.div(i, per_slab) + turned)
            place = jnp.where(k == 1, model * side + lax.rem(i, side), lax.rem(i, per_slab))
            return part_ref.at[k * slabs + s, at(place, piece)]

        def to_y(j):
            return remote(home(j, False), ry_ref.at[j], ys.at[lax.div(j, per_layer)], yr.at[j], ypeer)

        def issue(s, q):
            keep_out(s).wait()
            k, n = lax.div(s, slabs), lax.rem(s, slabs)
            for mine, fire, first, count in (
                    (k == 1, True, n * side, side), (k != 1, odd(n) == jnp.where(k == 0, 0, 1), lax.div(n, 2) * per_slab, per_slab)):
                for r in range(count):
                    j = k * per_layer + first + r
                    pl.when(mine & fire & (j < begun(q) + ahead))(lambda j=j: to_y(j).start())

        def to_x(j):
            return remote(mbuf.at[m_slot(j)], rx_ref.at[j], xs.at[m_slot(j)], xr.at[j], xpeer)

        def result(j, k):
            i = lax.rem(j, per_layer)
            if k == 1:
                return dw2_ref.at[at(c * side + lax.rem(i, side), piece), at(lax.div(i, side), width)]
            return (dw1_ref if k else dw3_ref).at[at(c * per_slab + lax.rem(i, per_slab), piece), at(lax.div(i, per_slab), width)]

        def put(j, k):
            slot = odd(j)
            return (copy(fbuf.at[slot], result(j, k), fs.at[slot]),
                    remote(fbuf.at[slot], result(j, k), fcs.at[slot], fcr.at[k], cpeer))

        def put_done(j):
            here_copy, there_copy = put(j, 0)
            here_copy.wait()
            there_copy.wait_send()

        def load_part(j, which):
            src = (lambda: ry_ref.at[j], lambda: home(j, True), lambda: rx_ref.at[j])[which]()
            return copy(src, ebuf.at[which], es.at[which])

        def fetch_x(j):
            to_x(j).wait_recv()
            load_part(j, 2).start()

        def begin(j, q):
            remote(ry_ref.at[j], ry_ref.at[j], ys.at[0], yr.at[j], ypeer).wait_recv()
            load_part(j, 0).start()
            load_part(j, 1).start()
            pl.when(j + ahead < sent_by(q))(lambda: to_y(j + ahead).start())
            pl.when(j >= 2)(lambda: fetch_x(j - 2))

        def deliver(j):
            load_part(j, 2).wait()
            pl.when(j >= 2)(lambda: put_done(j))
            fbuf[odd(j)] = mbuf[m_slot(j)] + ebuf[2]
            for k in range(n_layer):
                @pl.when(lax.div(j, per_layer) == k)
                def _(k=k):
                    for one in put(j, k):
                        one.start()

        def end(j):
            load_part(j, 0).wait()
            load_part(j, 1).wait()
            pl.when(j >= 4)(lambda: to_x(j).wait_send())
            mbuf[m_slot(j)] = ebuf[0] + ebuf[1]
            to_x(j).start()
            pl.when(j >= 2)(lambda: deliver(j - 2))

        def events(q):
            now, before, earlier = begun(q), begun(q - 1), begun(q - 2)
            pl.when(before > earlier)(lambda: end(before - 1))
            pl.when(now > before)(lambda: begin(now - 1, q))

        def weight_slab(k, n, v, d):
            slot = odd(k * slabs + n)
            for buf, part in ((psend, other(c)), (pkeep, c)):
                first = jnp.where(k == 1, part, 2 * part)
                for b in BOTH:
                    left = xbuf[at(first + b * jnp.where(k == 1, 2, 1), half // 2), pl.ds(v * rows, rows)]
                    here_at = at(b, half // 2)
                    prod = mm(left, d)
                    buf[slot, here_at] = buf[slot, here_at] + prod if v else prod

        def after(k, n, v, q):
            s = k * slabs + n
            if v == 0:
                pl.when(n > 0)(lambda: chip_sum(s - 1))
            else:
                pl.when(s >= 2)(lambda: pl.semaphore_wait(credit, 1))
                to_core(s).start()
                pl.when(n > 0)(lambda: issue(s - 1, q))

        def dw_pass(k, q, ready, fetch, pre, ahead_of_next):
            ready(0)
            fetch(1)
            pre(d0, 0, 0)

            def slab(n):
                for v, d_ref, d_next in ((0, d0, d1), (1, d1, d0)):
                    i = 2 * n + v
                    pl.when(i + 1 < items)(lambda: ready(i + 1))
                    pl.when(i + 2 < items)(lambda: fetch(i + 2))
                    pl.when(n == 0)(lambda: x_load(x2_ref, v).wait())
                    if v:
                        pl.when(n == slabs - 1)(ahead_of_next)
                    events(q + i)
                    for r in runs(rows, TM):
                        dbuf[pl.ds(v * rows + r.start, TM), at(column(k, n), width)] = d_ref[r]
                    weight_slab(k, n, v, d_ref[...])
                    pre(d_next, jnp.minimum(n + v, slabs - 1), other(v))
                    after(k, n, v, q + i)

            loop(slabs, slab)

        def emb_loads(i):
            n, v = split(i)
            cols = at(column(0, n), width)
            return (copy(d_ref.at[at(v, rows), cols], ubuf.at[v], us.at[v]),
                    copy(zh_ref.at[at(v, rows), cols], wbuf.at[v], ws.at[v]))

        def emb_fetch(i):
            for one in emb_loads(i):
                one.start()

        def emb_ready(i):
            for one in emb_loads(i):
                one.wait()

        def emb_pre(d_out, n, v):
            cols = at(column(0, n), width)
            _, inv = mean_inv(sz_ref[v, :, cols], total)
            sd = sd_ref[v, :, cols] / total
            for r in runs(rows, PIECE):
                d_out[r] = (inv * (ubuf[v, r] - sd[:1] - wbuf[v, r].astype(F32) * sd[1:])).astype(BF16)

        def x_load(src, v):
            return copy(src.at[:, at(v, rows)], xbuf.at[:, at(v, rows)], xl.at[v])

        def u_slot(layer, v):
            return jnp.where(layer == 0, other(v), v)

        def slab_of(ref, layer, i, buf, sem, slot):
            n, v = split(i)
            return copy(ref.at[at(v, rows), at(column(layer + 1, n), width)], buf.at[slot], sem.at[slot])

        def u_load(layer, i, ref=u2_ref):
            return slab_of(ref, layer, i, ubuf, us, u_slot(layer, odd(i)))

        def dy_load(layer, i):
            return slab_of(dy_ref, layer, i, dybuf, ds, odd(i))

        def dy_out(layer, i):
            n, v = split(i)
            return copy(dyout.at[v], dy_ref.at[at(v, rows), at(column(layer + 1, n), width)], dos.at[v])

        def w_load(layer, n, ref=w3_ref):
            slot = odd(n + 1)
            return copy(ref.at[:, at(column(layer + 1, n), width)], wbuf.at[slot], ws.at[slot])

        def by_layer(layer, make, refs):
            for k, ref in enumerate(refs):
                pl.when(layer == k)(lambda ref=ref: make(ref).start())

        def start_u(layer, i):
            by_layer(layer, lambda ref: u_load(layer, i, ref), (u2_ref, u1_ref))

        def start_w(layer, n):
            by_layer(layer, lambda ref: w_load(layer, n, ref), (w3_ref, w2_ref))

        def next_layer(layer):
            start_u(layer, 0)
            start_w(layer, 0)

        for one in (x_load(x2_ref, 0), *emb_loads(0), x_load(x2_ref, 1)):
            one.start()
        all_arrived()
        dw_pass(0, 0, emb_ready, emb_fetch, emb_pre, lambda: next_layer(0))

        def stats(layer, v, cols):
            pick = lambda one, two: jnp.where(layer == 0, one, two)
            mean, inv = mean_inv(pick(s2_ref[v, :, cols], s1_ref[v, :, cols]), total)
            gb = pick(gb2_ref[:, cols], gb1_ref[:, cols])
            return mean, inv, gb[:1], gb[1:]

        def bn_layer(layer):
            start = (2 * layer + 1) * items

            def dx_item(i):
                n, v = split(i)
                slot = u_slot(layer, v)
                cols = at(column(layer + 1, n), width)

                @pl.when(i + 1 < items)
                def _():
                    start_u(layer, i + 1)
                    pl.when((v == 0) & (n + 1 < slabs))(lambda: start_w(layer, n + 1))

                @pl.when(i + 1 == items)
                def _():
                    start_u(layer, 0)
                    dy_load(layer, 0).start()

                u_load(layer, i).wait()
                pl.when(v == 0)(lambda: w_load(layer, n).wait())
                events(start + i)
                pl.when((i == 4) | (i == 9))(lambda: by_layer(layer, lambda ref: x_load(ref, v), (x1_ref, h_ref)))
                pl.when(n > 0)(lambda: dy_out(layer, i).wait())
                mean, inv, gamma, beta = stats(layer, v, cols)

                def pieces():
                    for b in range(rows // TM):
                        dx = mm(dbuf[at(v * (rows // TM) + b, TM)], wbuf[odd(n + 1)])
                        for p in range(0, TM, PIECE):
                            some = pl.ds(b * TM + p, PIECE)
                            norm = (ubuf[slot, some] - mean) * inv
                            dy = jnp.where(norm * gamma + beta > 0, dx[p:p + PIECE], 0.0)
                            dyout[v, some] = dy
                            yield dy, dy * norm

                g = layer * items + i
                acc[g] = two_sums(pieces())
                dy_out(layer, i).start()
                share.start(g)
                before = (layer + 1) * slabs - 1
                pl.when(i == 0)(lambda: chip_sum(before))
                pl.when(i == 1)(lambda: issue(before, start + i))

            def fetch(i):
                start_u(layer, i)
                dy_load(layer, i).start()

            def ready(i):
                n, v = split(i)
                u_load(layer, i).wait()
                dy_load(layer, i).wait()
                sum_ref[layer, v, :, at(column(layer + 1, n), width)] = share.total(layer * items + i)

            def pre(d_out, n, v):
                cols = at(column(layer + 1, n), width)
                tot = sum_ref[layer, v, :, cols] / total
                mean, inv, gamma, _ = stats(layer, v, cols)
                slope, front, slot = inv * tot[1:], gamma * inv, u_slot(layer, v)
                for r in runs(rows, PIECE):
                    d_out[r] = (front * (dybuf[v, r] - (tot[:1] + (ubuf[slot, r] - mean) * slope))).astype(BF16)

            loop(items, dx_item)
            for v in BOTH:
                dy_out(layer, v).wait()
            dw_pass(layer + 1, start + items, ready, fetch, pre, lambda: pl.when(layer == 0)(lambda: next_layer(1)))

        loop(len(layers), bn_layer)

        ticks = (2 * n_layer - 1) * items
        chip_sum(n_slab - 1)
        issue(n_slab - 1, ticks)
        ended = 36

        def tail(j):
            begin(j, ticks + 2)
            end(j)

        loop(n_chunk, tail, ended)
        for j in range(n_chunk - 2, n_chunk):
            fetch_x(j)
            deliver(j)
        for j in BOTH:
            put_done(j)
        for k in range(n_layer):
            theirs = dw2_ref.at[at(other(c), half // 2)] if k == 1 else (dw1_ref if k else dw3_ref).at[at(other(c), half)]
            remote(theirs, theirs, fcs.at[0], fcr.at[k], cpeer).wait_recv()
            sent = ry_ref.at[at(k, per_layer)]
            remote(sent, sent, ys.at[k], yr.at[0], ypeer).wait_send()
        for j in range(n_chunk - 4, n_chunk):
            to_x(j).wait_send()

    n_item = len(layers) * items
    vm = lambda *shape: pltpu.VMEM(shape, F32)
    bf = lambda *shape: pltpu.VMEM(shape, BF16)
    return call(
        kernel, "backward", 4, (),
        [ANY, ANY, VMEM, VMEM] + [ANY] * 7 + [VMEM] * 4, [ANY] * 3 + [VMEM] + [ANY] * 4,
        [sds((dim, half), F32), sds((half, dim), F32), sds((dim, half), F32), sds((len(layers), 2, 2, dim), F32),
         sds((all_rows, dim), F32), sds((n_slab, half, width), F32), sds((n_chunk, piece, width), F32),
         sds((n_chunk, piece, width), F32)],
        [bf(all_rows, dim), bf(dim, all_rows), bf(rows, width), bf(rows, width), bf(2, dim, width),
         vm(2, rows, width), vm(2, rows, width), vm(2, rows, width),
         vm(2, half, width), vm(2, half, width), vm(2, half, width), vm(3, piece, width), vm(4, piece, width),
         vm(2, piece, width)] + Share.scratch(n_item, 2, width)
        + [TWO_DMA, TWO_DMA, TWO_DMA, TWO_DMA, TWO_DMA, DMA((n_slab,)), DMA((n_slab,)), DMA, DMA((n_layer,)),
           DMA((n_chunk,)), DMA((4,)), DMA((n_chunk,)), DMA((3,)), TWO_DMA, TWO_DMA, DMA((n_layer,)),
           pltpu.SemaphoreType.REGULAR],
        all_rows * dim * dim * 10, all_rows * dim * 40,
        (d_emb, zh, sz, s_emb, x2_t, x1_t, h_t, u2, u1, w3_t, w2_t, s2, s1, gb2, gb1))


def settle(*grads):
    steps = 8

    def kernel(*refs):
        for src, dst in zip(refs[:len(grads)], refs[len(grads):]):
            dst[...] = src[...]

    specs = [pl.BlockSpec((g.shape[0] // steps, g.shape[1]), lambda i: (i, 0)) for g in grads]
    return call(kernel, "settle", None, (steps,), specs, specs, [sds(g.shape, F32) for g in grads], [], 0,
                len(grads) * grads[0].size * 8, grads)


def solution(mesh):
    def shard_body(h_a, h_b, w_one, w_two, w_three, g_one, b_one, g_two, b_two, lam_off):
        y = lax.axis_index('model')
        total = float(h_a.shape[0] * mesh.shape['data'])
        dim, half = w_three.shape
        gb2 = jnp.stack([g_two, b_two])
        u1, s1, gb1, w_two_o, h_t = fwd_first(h_a, h_b, w_one, w_two, jnp.stack([g_one, b_one]))
        x1_t, u2, s2, w2_t, w_three_o = fwd_next(u1, s1, gb1, w_two, w_two_o, True, total, 1, w_three)
        x2_t, z, sz, w3_t = fwd_next(u2, s2, gb2, w_three, w_three_o, False, total, 2)
        zh, d_emb, s_emb, loss = corr_grad(z, sz, lam_off, total)
        loss = jnp.sum(loss)
        dw_three, dw_two, dw_one, sums, *_ = backward(
            d_emb.reshape(z.shape), zh.reshape(z.shape), sz, s_emb,
            ((u2, s2, gb2, w3_t, x1_t), (u1, s1, gb1, w2_t, h_t)), x2_t, total)
        dw_three, dw_two, dw_one = settle(dw_three, dw_two, dw_one)
        sums = jnp.sum(sums, axis=1)
        sum2 = sums[0]
        sum1 = lax.dynamic_slice_in_dim(sums[1], y * half, half, 1)
        return loss.reshape(1), dw_one, dw_two, dw_three, sum1[1], sum1[0], sum2[1], sum2[0]

    in_specs = (P('data', None), P('data', None), P(None, 'model'), P('model', None), P(None, 'model'),
                P('model'), P('model'), P(), P(), P())
    out_specs = (P(), P(None, 'model'), P('model', None), P(None, 'model'), P('model'), P('model'), P(), P())
    return jax.shard_map(shard_body, mesh=mesh, in_specs=in_specs, out_specs=out_specs, check_vma=False)
```

profile of v0, /device:TPU:0, one launch (start us, length us, event | category | flops | bytes accessed | tf_op | source)
XLA Modules:
  0.0 692.1 jit_solution(13302313047408840486)
XLA Ops:
  0.6 1.3 pad_maximum_fusion.1.gb_ref
  1.9 69.4 %fwd_first.1 = (f32[4096,2048]{1,0:T(8,128)}, f32[2,2,2048]{2,1,0:T(2,128)}, f32[2,2048]{1,0:T(2,128)}, bf16[1024,2048]{1,0:T(8,128)(2,1)}, bf16[2048,4096]{1,0:T(8,128)(2,1)}) custom-call(bf16[4096,2048]{1,0:T(8,128)(2,1)} %ha_ref.1, bf16[4096,2048]{1,0:T(8,128)(2,1)} %hb_ref.1, bf16[2048,1024]{1,0:T(8,128)(2,1)} %w_ref.1, bf16[1024,2048]{1,0:T(8,128)(2,1)} %wo_ref.2, ...), custom_call_target="tpu_custom_call" | custom-call | flops 34359738368 | bytes 100663296 | tf_op jit(solution)/shard_map/fwd_first/pallas_call | solution.py:215
  71.4 54.3 %fwd_next.2 = (bf16[2048,4096]{1,0:T(8,128)(2,1)}, f32[4096,2048]{1,0:T(8,128)}, f32[2,2,2048]{2,1,0:T(2,128)}, bf16[2048,2048]{1,0:T(8,128)(2,1)}, bf16[2048,1024]{1,0:T(8,128)(2,1)}) custom-call(f32[4096,2048]{1,0:T(8,128)} %get-tuple-element.33.u_ref.u1_ref, f32[2,2,2048]{2,1,0:T(2,128)} %get-tuple-element.34.s_ref.s1_ref, ...), custom_call_target="tpu_custom_call" | custom-call | flops 34359738368 | bytes 83886080 | tf_op jit(solution)/shard_map/fwd_next/pallas_call | solution.py:215
  125.7 1.3 pad_maximum_fusion.gb_ref.gb2_ref
  127.0 49.8 %fwd_next.3 = (bf16[2048,4096]{1,0:T(8,128)(2,1)}, f32[4096,2048]{1,0:T(8,128)}, f32[2,2,2048]{2,1,0:T(2,128)}, bf16[2048,2048]{1,0:T(8,128)(2,1)}) custom-call(f32[4096,2048]{1,0:T(8,128)} %get-tuple-element.37.u_ref.u2_ref, f32[2,2,2048]{2,1,0:T(2,128)} %get-tuple-element.38.s_ref.s2_ref, f32[2,2048]{1,0:T(2,128)} %pad_maximum_fusion.gb_ref.gb2_ref, ...), custom_call_target="tpu_custom_call" | custom-call | flops 34359738368 | bytes 83886080 | tf_op jit(solution)/shard_map/fwd_next/pallas_call | solution.py:215
  177.5 155.6 %corr_grad.1 = (bf16[2,2048,2048]{2,1,0:T(8,128)(2,1)}, f32[2,2048,2048]{2,1,0:T(8,128)}, f32[2,2,2048]{2,1,0:T(2,128)}, f32[1,128]{1,0:T(1,128)}) custom-call(f32[4096,2048]{1,0:T(8,128)} %get-tuple-element.40.z_ref, f32[2,2,2048]{2,1,0:T(2,128)} %get-tuple-element.41.s_ref.sz_ref, f32[1]{0:T(128)S(6)} %copy.18.lam_ref), custom_call_target="tpu_custom_call" | custom-call | flops 51539607552 | bytes 100663296 | tf_op jit(solution)/shard_map/corr_grad/pallas_call | solution.py:215
  333.0 1.3 reduce_sum.18
  334.3 337.6 %backward.1 = (f32[2048,1024]{1,0:T(8,128)}, f32[1024,2048]{1,0:T(8,128)}, f32[2048,1024]{1,0:T(8,128)}, f32[2,2,2,2048]{3,2,1,0:T(2,128)}, f32[4096,2048]{1,0:T...) custom-call(f32[4096,2048]{1,0:T(8,128)} %bitcast.19, ...), custom_call_target="tpu_custom_call" | custom-call | flops 171798691840 | bytes 335544320 | tf_op jit(solution)/shard_map/backward/pallas_call | solution.py:215
  671.9 18.1 %settle.1 = (f32[2048,1024]{1,0:T(8,128)}, f32[1024,2048]{1,0:T(8,128)}, f32[2048,1024]{1,0:T(8,128)}) custom-call(f32[2048,1024]{1,0:T(8,128)} %get-tuple-element.51.refs_0_, f32[1024,2048]{1,0:T(8,128)} %get-tuple-element.52.refs_1_, f32[2048,1024]{1,0:T(8,128)} %get-tuple-element.53.refs_2_), custom_call_target="tpu_custom_call" | custom-call | bytes 50331648 | tf_op jit(solution)/shard_map/settle/pallas_call | solution.py:215
  689.9 0.9 reduce_sum.19
  690.8 0.7 constant_dynamic-slice_fusion.1
  691.5 0.6 fusion
  (1 shorter events, 0.0 us)
where the time goes:
time: 694 us; the launch traced here: 692 us
  Pallas kernels  685 us (99%)
    pallas_call x6, Pallas kernels, call(): pl.pallas_call(kernel, name=name, grid=grid, in_specs=in_specs, out_specs...  685 us

commit v1 on v0

--- a/solution.py
+++ b/solution.py
@@ -218,7 +218,7 @@
         cost_estimate=pl.CostEstimate(flops=flops, bytes_accessed=nbytes, transcendentals=0))(*args)
 
 
-def fwd_first(h_a, h_b, w_one, w_two, gb_own):
+def fwd_first(h_a, h_b, w_one, w_two, *vectors):
     depth, half = w_one.shape
     dim = 2 * half
     rows = h_a.shape[0] // 2
@@ -234,7 +234,8 @@
     def tile_of(j, i):
         return jnp.where(odd(j) == 0, i, per_block - 1 - i)
 
-    def kernel(ha_ref, hb_ref, w_ref, w2_ref, gb_ref, u_ref, s_ref, gbo_ref, w2o_ref, ht_ref, w1, gbf, *sems):
+    def kernel(ha_ref, hb_ref, w_ref, w2_ref, g1_ref, b1_ref, g2_ref, b2_ref, u_ref, s_ref, gbo_ref, gb2_ref, w2o_ref, ht_ref,
+               w1, gbf, *sems):
         share, sems = Share(*sems[:4]), sems[4:]
         gs, gr, lsem = sems[:3]
         sems = sems[3:]
@@ -251,7 +252,7 @@
             return pltpu.make_async_copy(w_ref.at[:, at(b, width)], w1.at[:, at(2 * y + b, width)], lsem.at[b])
 
         def bn_vectors(m):
-            return remote(gb_ref, gbf.at[:, at(m, half)], gs, gr, flip(here, Y_PEER))
+            return remote(gbf.at[:, at(m, half)], gbf.at[:, at(m, half)], gs, gr, flip(here, Y_PEER))
 
         def begin():
             arrive()
@@ -260,7 +261,10 @@
             all_arrived()
             one.start()
             two.start()
-            bn_vectors(y).start()
+            for r, (one_ref, two_ref) in enumerate(((g1_ref, g2_ref), (b1_ref, b2_ref))):
+                row = pl.ds(r, 1)
+                gbf[row, at(y, half)] = one_ref[...]
+                gb2_ref[row] = two_ref[...]
             local(0).wait()
 
         def late_half():
@@ -268,7 +272,7 @@
             one.pass_y(n - 1)
             one.wait_core(0)
 
-        hooks = [(0, begin), (per_block, lambda: local(1).wait()), (2 * per_block, late_half)]
+        hooks = [(0, begin), (1, lambda: bn_vectors(y).start()), (per_block, lambda: local(1).wait()), (2 * per_block, late_half)]
         hooks += [(2 * p + 3, functools.partial(one.pass_y, p)) for p in range(n - 1)]
         hooks += [(p + 2 * per_block, functools.partial(one.pass_x, p)) for p in range(1, n)]
         hooks += [(3 * per_block, lambda: one.wait_core(1))]
@@ -298,7 +302,6 @@
             bn_vectors(other(y)).wait_recv()
             bn_vectors(y).wait_send()
             gbo_ref[...] = gbf[...]
-            gbo_ref[:, at(y, half)] = gb_ref[...]
             for b in range(4):
                 s_ref[:, :, b * width:(b + 1) * width] = share.total(b)
             one.drain()
@@ -310,14 +313,14 @@
         kernel, "fwd_first", 0, (4, per_block),
         [pl.BlockSpec((tile, depth), lambda j, i: (coords()[0] * steps + jnp.minimum(tile_of(j, i), steps - 1), 0)),
          pl.BlockSpec((tile, depth), lambda j, i: (coords()[0] * steps + jnp.maximum(tile_of(j, i) - steps, 0), 0)),
-         ANY, ANY, whole(2, half)],
+         ANY, ANY] + [whole(*t.shape) for t in vectors],
         [pl.BlockSpec((tile, width), lambda j, i: (tile_of(j, i), block(j))), whole(2, 2, dim),
-         whole(2, dim), ANY, pl.BlockSpec((width, tile), lambda j, i: (j, tile_of(j, i)))],
-        [sds((2 * rows, dim), F32), sds((2, 2, dim), F32), sds((2, dim), F32), sds((half, dim), BF16),
-         sds((depth, 2 * rows), BF16)],
+         whole(2, dim), whole(2, dim), ANY, pl.BlockSpec((width, tile), lambda j, i: (j, tile_of(j, i)))],
+        [sds((2 * rows, dim), F32), sds((2, 2, dim), F32), sds((2, dim), F32), sds((2, dim), F32),
+         sds((half, dim), BF16), sds((depth, 2 * rows), BF16)],
         [pltpu.VMEM((depth, dim), BF16), pltpu.VMEM((2, dim), F32)] + Share.scratch(4, 2, 2, width)
         + [DMA, DMA, TWO_DMA] + Gather.scratch(n) + Gather.scratch(n2),
-        4 * rows * depth * dim, 2 * rows * (8 * depth + 4 * dim), (h_a, h_b, w_one, w_two, gb_own))
+        4 * rows * depth * dim, 2 * rows * (8 * depth + 4 * dim), (h_a, h_b, w_one, w_two, *vectors))
 
 
 def fwd_next(u, sums, gb, w_own, w_other, by_rows, total, cid, w_next=None):
@@ -329,12 +332,13 @@
     last = 2 * steps - 1
     slab = dim // (2 * steps)
     n = 4
+    more = w_next is not None
 
     def kernel(u_ref, s_ref, gb_ref, wo_ref, wt_ref, *refs):
-        if w_next is not None:
+        if more:
             wn_ref, refs = refs[0], refs[1:]
         x_ref, o_ref, so_ref, wtr_ref, *refs = refs
-        if w_next is not None:
+        if more:
             wno_ref, *refs = refs
         w, act, acc, got, ssem, rsem, lsem, *refs = refs
         share = Share(acc, got, ssem, rsem)
@@ -345,7 +349,7 @@
             where = at(model, half)
             return pltpu.make_async_copy(ref, w.at[where] if by_rows else w.at[:, where], lsem.at[b])
 
-        if w_next is not None:
+        if more:
             gather = Gather(lambda q, p: wn_ref.at[at(p, depth // n), at(q, quarter)],
                             lambda m, q, p: wno_ref.at[at(p, depth // n), at(q, quarter)], n, refs)
 
@@ -356,15 +360,15 @@
             local(wo_ref, y, 0).start()
             local(wt_ref, other(y), 1).start()
             all_arrived()
-            if w_next is not None:
+            if more:
                 gather.start()
             local(wo_ref, y, 0).wait()
             local(wt_ref, other(y), 1).wait()
 
-        if w_next is not None:
+        if more:
             for p in range(n):
-                pl.when(i == p + 1)(lambda p=p: gather.pass_y(p))
-                pl.when(i == p + 3)(lambda p=p: gather.pass_x(p))
+                pl.when(i == p + 2)(lambda p=p: gather.pass_y(p))
+                pl.when(i == p + 4)(lambda p=p: gather.pass_x(p))
         pl.when(i == steps)(lambda: share.start(0))
 
         mean, inv = mean_inv(s_ref[0], total)
@@ -387,12 +391,11 @@
             share.start(1)
             for b in BOTH:
                 so_ref[b] = share.total(b)
-            if w_next is not None:
+            if more:
                 gather.drain()
                 gather.wait_core(0)
                 gather.wait_core(1)
 
-    more = w_next is not None
     return call(
         kernel, "fwd_next", cid, (2 * steps,),
         [pl.BlockSpec((TM, depth), lambda i: (i, 0)), pl.BlockSpec((1, 2, depth), lambda i: (i // steps, 0, 0)),
@@ -417,7 +420,7 @@
     mt = TM
     zt = TM // 2
     ahead = 3
-    lead = 4
+    lead = 3
     z_steps = all_rows // zt
     m_steps = rows // mt
     scale = 1.0 / total
@@ -495,7 +498,7 @@
             to_core(t).wait_recv()
             to_core(t).wait_send()
             ck[:, at(t, pair)] += drecv[odd(t)]
-            pl.when(t < lead - 1)(lambda: to_first(t).start())
+            to_first(t).start()
 
         def corr_part(t):
             zh_out(t).start()
@@ -567,7 +570,6 @@
         def back_second(t):
             g_second(t, other(bit2)).wait_recv()
             g_first(t, bit1).start()
-            pl.when(t + lead - 1 < n_chunk)(lambda: to_first(t + lead - 1).start())
 
         def back_first(t):
             g_first(t, other(bit1)).wait_recv()
@@ -578,12 +580,12 @@
             grads(t)
 
         def advance(tau):
-            for lag, stage_fn in ((lead, at_first), (lead + 2, back_core), (lead + 1, back_first), (lead, at_second),
-                                  (1, chip_sum), (0, corr_part), (lead, back_second)):
+            for lag, stage_fn in ((lead, at_first), (lead + 1, back_second), (lead + 2, back_first), (lead + 3, back_core),
+                                  (lead, at_second), (1, chip_sum), (0, corr_part)):
                 t = tau - lag
                 pl.when(jnp.logical_and(t >= 0, t < n_chunk))(lambda t=t, stage_fn=stage_fn: stage_fn(t))
 
-        loop(n_chunk + lead + 2, advance)
+        loop(n_chunk + lead + 3, advance)
         share.start(1)
         share.start(0)
         for t in range(n_chunk):
@@ -815,8 +817,8 @@
             for r in runs(rows, PIECE):
                 d_out[r] = (inv * (ubuf[v, r] - sd[:1] - wbuf[v, r].astype(F32) * sd[1:])).astype(BF16)
 
-        def x_load(src, v):
-            return copy(src.at[:, at(v, rows)], xbuf.at[:, at(v, rows)], xl.at[v])
+        def x_load(src, v, rows_at=pl.ds(0, dim)):
+            return copy(src.at[rows_at, at(v, rows)], xbuf.at[rows_at, at(v, rows)], xl.at[v])
 
         def u_slot(layer, v):
             return jnp.where(layer == 0, other(v), v)
@@ -885,7 +887,8 @@
                 u_load(layer, i).wait()
                 pl.when(v == 0)(lambda: w_load(layer, n).wait())
                 events(start + i)
-                pl.when((i == 4) | (i == 9))(lambda: by_layer(layer, lambda ref: x_load(ref, v), (x1_ref, h_ref)))
+                pl.when((i > 2) & (i < 11))(lambda: by_layer(
+                    layer, lambda ref: x_load(ref, v, at(lax.div(i - 3, 2), half // 2)), (x1_ref, h_ref)))
                 pl.when(n > 0)(lambda: dy_out(layer, i).wait())
                 mean, inv, gamma, beta = stats(layer, v, cols)
 
@@ -976,7 +979,7 @@
 
 
 def settle(*grads):
-    steps = 8
+    steps = 16
 
     def kernel(*refs):
         for src, dst in zip(refs[:len(grads)], refs[len(grads):]):
@@ -992,8 +995,8 @@
         y = lax.axis_index('model')
         total = float(h_a.shape[0] * mesh.shape['data'])
         dim, half = w_three.shape
-        gb2 = jnp.stack([g_two, b_two])
-        u1, s1, gb1, w_two_o, h_t = fwd_first(h_a, h_b, w_one, w_two, jnp.stack([g_one, b_one]))
+        rowed = [t.reshape(1, -1) for t in (g_one, b_one, g_two, b_two)]
+        u1, s1, gb1, gb2, w_two_o, h_t = fwd_first(h_a, h_b, w_one, w_two, *rowed)
         x1_t, u2, s2, w2_t, w_three_o = fwd_next(u1, s1, gb1, w_two, w_two_o, True, total, 1, w_three)
         x2_t, z, sz, w3_t = fwd_next(u2, s2, gb2, w_three, w_three_o, False, total, 2)
         zh, d_emb, s_emb, loss = corr_grad(z, sz, lam_off, total)

time: 694 us -> 685 us (0.987)
  Pallas kernels: 685 us -> 678 us
where the time goes in v1:
time: 685 us; the launch traced here: 683 us
  Pallas kernels  678 us (99%)
    pallas_call x6, Pallas kernels, call(): pl.pallas_call(kernel, name=name, grid=grid, in_specs=in_specs, out_specs...  678 us

profile of v1, /device:TPU:0, one launch (start us, length us, event | category | flops | bytes accessed | tf_op | source)
XLA Modules:
  0.0 682.7 jit_solution(6072076685975207669)
XLA Ops:
  0.6 69.6 %fwd_first.1 = (f32[4096,2048]{1,0:T(8,128)}, f32[2,2,2048]{2,1,0:T(2,128)}, f32[2,2048]{1,0:T(2,128)}, f32[2,2048]{1,0:T(2,128)}, bf16[1024,2048]{1,0:T(8,128)(2,1)}, /*index=5*/bf16[2048,4096]{1,0:T(8,128)(2,1)}) custom-call(bf16[4096,2048]{1,0:T(8,128)(2,1)} %ha_ref.1, bf16[4096,2048]{1,0:T(8,128)(2,1)} %hb_ref.1, bf16[2048,1024]{1,0:T(8,128)(2,1)} %w_ref.1, ...), custom_call_target="tpu_custom_call" | custom-call | flops 34359738368 | bytes 100663296 | tf_op jit(solution)/shard_map/fwd_first/pallas_call | solution.py:215
  70.2 53.5 %fwd_next.2 = (bf16[2048,4096]{1,0:T(8,128)(2,1)}, f32[4096,2048]{1,0:T(8,128)}, f32[2,2,2048]{2,1,0:T(2,128)}, bf16[2048,2048]{1,0:T(8,128)(2,1)}, bf16[2048,1024]{1,0:T(8,128)(2,1)}) custom-call(f32[4096,2048]{1,0:T(8,128)} %get-tuple-element.34.u_ref.u1_ref, f32[2,2,2048]{2,1,0:T(2,128)} %get-tuple-element.35.s_ref.s1_ref, ...), custom_call_target="tpu_custom_call" | custom-call | flops 34359738368 | bytes 83886080 | tf_op jit(solution)/shard_map/fwd_next/pallas_call | solution.py:215
  123.7 49.7 %fwd_next.3 = (bf16[2048,4096]{1,0:T(8,128)(2,1)}, f32[4096,2048]{1,0:T(8,128)}, f32[2,2,2048]{2,1,0:T(2,128)}, bf16[2048,2048]{1,0:T(8,128)(2,1)}) custom-call(f32[4096,2048]{1,0:T(8,128)} %get-tuple-element.38.u_ref.u2_ref, f32[2,2,2048]{2,1,0:T(2,128)} %get-tuple-element.39.s_ref.s2_ref, f32[2,2048]{1,0:T(2,128)} %get-tuple-element.40.gb_ref.gb2_ref, ...), custom_call_target="tpu_custom_call" | custom-call | flops 34359738368 | bytes 83886080 | tf_op jit(solution)/shard_map/fwd_next/pallas_call | solution.py:215
  174.1 149.5 %corr_grad.1 = (bf16[2,2048,2048]{2,1,0:T(8,128)(2,1)}, f32[2,2048,2048]{2,1,0:T(8,128)}, f32[2,2,2048]{2,1,0:T(2,128)}, f32[1,128]{1,0:T(1,128)}) custom-call(f32[4096,2048]{1,0:T(8,128)} %get-tuple-element.42.z_ref, f32[2,2,2048]{2,1,0:T(2,128)} %get-tuple-element.43.s_ref.sz_ref, f32[1]{0:T(128)S(6)} %copy.18.lam_ref), custom_call_target="tpu_custom_call" | custom-call | flops 51539607552 | bytes 100663296 | tf_op jit(solution)/shard_map/corr_grad/pallas_call | solution.py:215
  323.7 1.3 reduce_sum.18
  324.9 333.6 %backward.1 = (f32[2048,1024]{1,0:T(8,128)}, f32[1024,2048]{1,0:T(8,128)}, f32[2048,1024]{1,0:T(8,128)}, f32[2,2,2,2048]{3,2,1,0:T(2,128)}, f32[4096,2048]{1,0:T...) custom-call(f32[4096,2048]{1,0:T(8,128)} %bitcast.19, ...), custom_call_target="tpu_custom_call" | custom-call | flops 171798691840 | bytes 335544320 | tf_op jit(solution)/shard_map/backward/pallas_call | solution.py:215
  658.5 22.0 %settle.1 = (f32[2048,1024]{1,0:T(8,128)}, f32[1024,2048]{1,0:T(8,128)}, f32[2048,1024]{1,0:T(8,128)}) custom-call(f32[2048,1024]{1,0:T(8,128)} %get-tuple-element.53.refs_0_, f32[1024,2048]{1,0:T(8,128)} %get-tuple-element.54.refs_1_, f32[2048,1024]{1,0:T(8,128)} %get-tuple-element.55.refs_2_), custom_call_target="tpu_custom_call" | custom-call | bytes 50331648 | tf_op jit(solution)/shard_map/settle/pallas_call | solution.py:215
  680.5 0.9 reduce_sum.19
  681.4 0.7 constant_dynamic-slice_fusion.1
  682.1 0.6 fusion
  (1 shorter events, 0.0 us)

commit v2 on v1

--- a/solution.py
+++ b/solution.py
@@ -630,7 +630,7 @@
 
     def kernel(d_ref, zh_ref, sz_ref, sd_ref, x2_ref, x1_ref, h_ref, u2_ref, u1_ref, w3_ref, w2_ref,
                s2_ref, s1_ref, gb2_ref, gb1_ref, dw3_ref, dw2_ref, dw1_ref, sum_ref, dy_ref, part_ref, ry_ref, rx_ref,
-               dbuf, xbuf, d0, d1, wbuf, ubuf, dybuf, dyout, psend, pkeep, dr, ebuf, mbuf, fbuf, acc, got, ssem, rsem,
+               dbuf, xbuf, wbuf, ubuf, dybuf, dyout, psend, pkeep, dr, ebuf, mbuf, fbuf, acc, got, ssem, rsem,
                us, ws, ds, dos, xl, ps, pr, pm, ys, yr, xs, xr, es, fs, fcs, fcr, credit):
         share = Share(acc, got, ssem, rsem)
         here = coords()
@@ -775,24 +775,18 @@
                 pl.when(n > 0)(lambda: issue(s - 1, q))
 
         def dw_pass(k, q, ready, fetch, pre, ahead_of_next):
-            ready(0)
-            fetch(1)
-            pre(d0, 0, 0)
-
             def slab(n):
-                for v, d_ref, d_next in ((0, d0, d1), (1, d1, d0)):
+                for v in BOTH:
                     i = 2 * n + v
-                    pl.when(i + 1 < items)(lambda: ready(i + 1))
-                    pl.when(i + 2 < items)(lambda: fetch(i + 2))
+                    pl.when(i + 1 < items)(lambda: fetch(i + 1))
+                    ready(i)
                     pl.when(n == 0)(lambda: x_load(x2_ref, v).wait())
-                    if v:
-                        pl.when(n == slabs - 1)(ahead_of_next)
                     events(q + i)
-                    for r in runs(rows, TM):
-                        dbuf[pl.ds(v * rows + r.start, TM), at(column(k, n), width)] = d_ref[r]
-                    weight_slab(k, n, v, d_ref[...])
-                    pre(d_next, jnp.minimum(n + v, slabs - 1), other(v))
+                    cols = at(column(k, n), width)
+                    pre(v * rows, cols, v)
+                    weight_slab(k, n, v, dbuf[pl.ds(v * rows, rows), cols])
                     after(k, n, v, q + i)
+                pl.when(n == slabs - 1)(ahead_of_next)
 
             loop(slabs, slab)
 
@@ -810,12 +804,12 @@
             for one in emb_loads(i):
                 one.wait()
 
-        def emb_pre(d_out, n, v):
-            cols = at(column(0, n), width)
+        def emb_pre(row, cols, v):
             _, inv = mean_inv(sz_ref[v, :, cols], total)
             sd = sd_ref[v, :, cols] / total
             for r in runs(rows, PIECE):
-                d_out[r] = (inv * (ubuf[v, r] - sd[:1] - wbuf[v, r].astype(F32) * sd[1:])).astype(BF16)
+                dbuf[pl.ds(row + r.start, PIECE), cols] = (
+                    inv * (ubuf[v, r] - sd[:1] - wbuf[v, r].astype(F32) * sd[1:])).astype(BF16)
 
         def x_load(src, v, rows_at=pl.ds(0, dim)):
             return copy(src.at[rows_at, at(v, rows)], xbuf.at[rows_at, at(v, rows)], xl.at[v])
@@ -893,10 +887,10 @@
                 mean, inv, gamma, beta = stats(layer, v, cols)
 
                 def pieces():
-                    for b in range(rows // TM):
-                        dx = mm(dbuf[at(v * (rows // TM) + b, TM)], wbuf[odd(n + 1)])
-                        for p in range(0, TM, PIECE):
-                            some = pl.ds(b * TM + p, PIECE)
+                    for b in BOTH:
+                        dx = mm(dbuf[at(2 * v + b, rows // 2)], wbuf[odd(n + 1)])
+                        for p in range(0, rows // 2, PIECE):
+                            some = pl.ds(b * (rows // 2) + p, PIECE)
                             norm = (ubuf[slot, some] - mean) * inv
                             dy = jnp.where(norm * gamma + beta > 0, dx[p:p + PIECE], 0.0)
                             dyout[v, some] = dy
@@ -920,13 +914,13 @@
                 dy_load(layer, i).wait()
                 sum_ref[layer, v, :, at(column(layer + 1, n), width)] = share.total(layer * items + i)
 
-            def pre(d_out, n, v):
-                cols = at(column(layer + 1, n), width)
+            def pre(row, cols, v):
                 tot = sum_ref[layer, v, :, cols] / total
                 mean, inv, gamma, _ = stats(layer, v, cols)
                 slope, front, slot = inv * tot[1:], gamma * inv, u_slot(layer, v)
                 for r in runs(rows, PIECE):
-                    d_out[r] = (front * (dybuf[v, r] - (tot[:1] + (ubuf[slot, r] - mean) * slope))).astype(BF16)
+                    dbuf[pl.ds(row + r.start, PIECE), cols] = (
+                        front * (dybuf[v, r] - (tot[:1] + (ubuf[slot, r] - mean) * slope))).astype(BF16)
 
             loop(items, dx_item)
             for v in BOTH:
@@ -961,14 +955,13 @@
     n_item = len(layers) * items
     vm = lambda *shape: pltpu.VMEM(shape, F32)
     bf = lambda *shape: pltpu.VMEM(shape, BF16)
-    return call(
+    outs = call(
         kernel, "backward", 4, (),
         [ANY, ANY, VMEM, VMEM] + [ANY] * 7 + [VMEM] * 4, [ANY] * 3 + [VMEM] + [ANY] * 4,
         [sds((dim, half), F32), sds((half, dim), F32), sds((dim, half), F32), sds((len(layers), 2, 2, dim), F32),
          sds((all_rows, dim), F32), sds((n_slab, half, width), F32), sds((n_chunk, piece, width), F32),
          sds((n_chunk, piece, width), F32)],
-        [bf(all_rows, dim), bf(dim, all_rows), bf(rows, width), bf(rows, width), bf(2, dim, width),
-         vm(2, rows, width), vm(2, rows, width), vm(2, rows, width),
+        [bf(all_rows, dim), bf(dim, all_rows), bf(2, dim, width), vm(2, rows, width), vm(2, rows, width), vm(2, rows, width),
          vm(2, half, width), vm(2, half, width), vm(2, half, width), vm(3, piece, width), vm(4, piece, width),
          vm(2, piece, width)] + Share.scratch(n_item, 2, width)
         + [TWO_DMA, TWO_DMA, TWO_DMA, TWO_DMA, TWO_DMA, DMA((n_slab,)), DMA((n_slab,)), DMA, DMA((n_layer,)),
@@ -976,39 +969,48 @@
            pltpu.SemaphoreType.REGULAR],
         all_rows * dim * dim * 10, all_rows * dim * 40,
         (d_emb, zh, sz, s_emb, x2_t, x1_t, h_t, u2, u1, w3_t, w2_t, s2, s1, gb2, gb1))
-
-
-def settle(*grads):
-    steps = 16
-
-    def kernel(*refs):
-        for src, dst in zip(refs[:len(grads)], refs[len(grads):]):
+    return outs[:n_layer + 1]
+
+
+def settle(grads, sums, loss):
+    steps = 4
+    dim = sums.shape[-1]
+    half = dim // 2
+
+    def kernel(sum_ref, loss_ref, src3, src2, src1, g2_ref, b2_ref, g1_ref, b1_ref, total_ref, *dsts):
+        for src, dst in zip((src3, src2, src1), dsts):
             dst[...] = src[...]
 
+        @pl.when(pl.program_id(0) == 0)
+        def _():
+            y, _, _ = coords()
+            for layer, (cols, g_ref, b_ref) in enumerate(((pl.ds(0, dim), g2_ref, b2_ref), (at(y, half), g1_ref, b1_ref))):
+                both = jnp.sum(sum_ref[layer, :, :, cols], axis=0)
+                g_ref[...] = both[1:]
+                b_ref[...] = both[:1]
+            total_ref[...] = jnp.sum(loss_ref[...], axis=1, keepdims=True)
+
     specs = [pl.BlockSpec((g.shape[0] // steps, g.shape[1]), lambda i: (i, 0)) for g in grads]
-    return call(kernel, "settle", None, (steps,), specs, specs, [sds(g.shape, F32) for g in grads], [], 0,
-                len(grads) * grads[0].size * 8, grads)
+    small = [(1, n) for n in (dim, dim, half, half, 1)]
+    return call(kernel, "settle", None, (steps,), [whole(*sums.shape), whole(*loss.shape)] + specs,
+                [whole(*t) for t in small] + specs, [sds(t, F32) for t in small] + [sds(g.shape, F32) for g in grads], [], 0,
+                sum(g.size for g in grads) * 8, (sums, loss, *grads))
 
 
 def solution(mesh):
     def shard_body(h_a, h_b, w_one, w_two, w_three, g_one, b_one, g_two, b_two, lam_off):
-        y = lax.axis_index('model')
         total = float(h_a.shape[0] * mesh.shape['data'])
-        dim, half = w_three.shape
         rowed = [t.reshape(1, -1) for t in (g_one, b_one, g_two, b_two)]
         u1, s1, gb1, gb2, w_two_o, h_t = fwd_first(h_a, h_b, w_one, w_two, *rowed)
         x1_t, u2, s2, w2_t, w_three_o = fwd_next(u1, s1, gb1, w_two, w_two_o, True, total, 1, w_three)
         x2_t, z, sz, w3_t = fwd_next(u2, s2, gb2, w_three, w_three_o, False, total, 2)
         zh, d_emb, s_emb, loss = corr_grad(z, sz, lam_off, total)
-        loss = jnp.sum(loss)
-        dw_three, dw_two, dw_one, sums, *_ = backward(
+        *grads, sums = backward(
             d_emb.reshape(z.shape), zh.reshape(z.shape), sz, s_emb,
             ((u2, s2, gb2, w3_t, x1_t), (u1, s1, gb1, w2_t, h_t)), x2_t, total)
-        dw_three, dw_two, dw_one = settle(dw_three, dw_two, dw_one)
-        sums = jnp.sum(sums, axis=1)
-        sum2 = sums[0]
-        sum1 = lax.dynamic_slice_in_dim(sums[1], y * half, half, 1)
-        return loss.reshape(1), dw_one, dw_two, dw_three, sum1[1], sum1[0], sum2[1], sum2[0]
+        *small, dw_three, dw_two, dw_one = settle(grads, sums, loss)
+        dg_two, db_two, dg_one, db_one, loss = (t.reshape(-1) for t in small)
+        return loss, dw_one, dw_two, dw_three, dg_one, db_one, dg_two, db_two
 
     in_specs = (P('data', None), P('data', None), P(None, 'model'), P('model', None), P(None, 'model'),
                 P('model'), P('model'), P(), P(), P())

time: 685 us -> 657 us (0.959)
  Pallas kernels: 678 us -> 654 us
    pallas_call x6, Pallas kernels: 678 us -> 654 us  [call(): pl.pallas_call(kernel, name=name, grid=grid, in_specs=in_specs, out_specs...]
where the time goes in v2:
time: 657 us; the launch traced here: 655 us
  Pallas kernels  654 us (100%)
    pallas_call x6, Pallas kernels, call(): pl.pallas_call(kernel, name=name, grid=grid, in_specs=in_specs, out_specs...  654 us

profile of v2, /device:TPU:0, one launch (start us, length us, event | category | flops | bytes accessed | tf_op | source)
XLA Modules:
  0.0 655.1 jit_solution(15179480322320956719)
XLA Ops:
  1.3 69.6 %fwd_first.1 = (f32[4096,2048]{1,0:T(8,128)}, f32[2,2,2048]{2,1,0:T(2,128)}, f32[2,2048]{1,0:T(2,128)}, f32[2,2048]{1,0:T(2,128)}, bf16[1024,2048]{1,0:T(8,128)(2,1)}, /*index=5*/bf16[2048,4096]{1,0:T(8,128)(2,1)}) custom-call(bf16[4096,2048]{1,0:T(8,128)(2,1)} %ha_ref.1, bf16[4096,2048]{1,0:T(8,128)(2,1)} %hb_ref.1, bf16[2048,1024]{1,0:T(8,128)(2,1)} %w_ref.1, ...), custom_call_target="tpu_custom_call" | custom-call | flops 34359738368 | bytes 100663296 | tf_op jit(solution)/shard_map/fwd_first/pallas_call | solution.py:215
  70.9 53.4 %fwd_next.2 = (bf16[2048,4096]{1,0:T(8,128)(2,1)}, f32[4096,2048]{1,0:T(8,128)}, f32[2,2,2048]{2,1,0:T(2,128)}, bf16[2048,2048]{1,0:T(8,128)(2,1)}, bf16[2048,1024]{1,0:T(8,128)(2,1)}) custom-call(f32[4096,2048]{1,0:T(8,128)} %get-tuple-element.39.u_ref.u1_ref, f32[2,2,2048]{2,1,0:T(2,128)} %get-tuple-element.40.s_ref.s1_ref, ...), custom_call_target="tpu_custom_call" | custom-call | flops 34359738368 | bytes 83886080 | tf_op jit(solution)/shard_map/fwd_next/pallas_call | solution.py:215
  124.3 50.0 %fwd_next.3 = (bf16[2048,4096]{1,0:T(8,128)(2,1)}, f32[4096,2048]{1,0:T(8,128)}, f32[2,2,2048]{2,1,0:T(2,128)}, bf16[2048,2048]{1,0:T(8,128)(2,1)}) custom-call(f32[4096,2048]{1,0:T(8,128)} %get-tuple-element.43.u_ref.u2_ref, f32[2,2,2048]{2,1,0:T(2,128)} %get-tuple-element.44.s_ref.s2_ref, f32[2,2048]{1,0:T(2,128)} %get-tuple-element.45.gb_ref.gb2_ref, ...), custom_call_target="tpu_custom_call" | custom-call | flops 34359738368 | bytes 83886080 | tf_op jit(solution)/shard_map/fwd_next/pallas_call | solution.py:215
  174.3 149.6 %corr_grad.1 = (bf16[2,2048,2048]{2,1,0:T(8,128)(2,1)}, f32[2,2048,2048]{2,1,0:T(8,128)}, f32[2,2,2048]{2,1,0:T(2,128)}, f32[1,128]{1,0:T(1,128)}) custom-call(f32[4096,2048]{1,0:T(8,128)} %get-tuple-element.47.z_ref, f32[2,2,2048]{2,1,0:T(2,128)} %get-tuple-element.48.s_ref.sz_ref, f32[1]{0:T(128)S(6)} %copy.18.lam_ref), custom_call_target="tpu_custom_call" | custom-call | flops 51539607552 | bytes 100663296 | tf_op jit(solution)/shard_map/corr_grad/pallas_call | solution.py:215
  323.9 315.0 %backward.1 = (f32[2048,1024]{1,0:T(8,128)}, f32[1024,2048]{1,0:T(8,128)}, f32[2048,1024]{1,0:T(8,128)}, f32[2,2,2,2048]{3,2,1,0:T(2,128)}, f32[4096,2048]{1,0:T...) custom-call(f32[4096,2048]{1,0:T(8,128)} %bitcast.19, ...), custom_call_target="tpu_custom_call" | custom-call | flops 171798691840 | bytes 335544320 | tf_op jit(solution)/shard_map/backward/pallas_call | solution.py:215
  638.9 16.2 %settle.1 = (f32[1,2048]{1,0:T(1,128)}, f32[1,2048]{1,0:T(1,128)}, f32[1,1024]{1,0:T(1,128)}, f32[1,1024]{1,0:T(1,128)}, f32[1,1]{1,0:T(1,128)}, /*index=5*/f32[...) custom-call(f32[2,2,2,2048]{3,2,1,0:T(2,128)} %get-tuple-element.57.sum_ref, ...), custom_call_target="tpu_custom_call" | custom-call | bytes 50331648 | tf_op jit(solution)/shard_map/settle/pallas_call | solution.py:215

commit v3 on v2

--- a/solution.py
+++ b/solution.py
@@ -417,8 +417,8 @@
     n_chunk = 8
     width = half // n_chunk
     pair = 2 * width
-    mt = TM
-    zt = TM // 2
+    mt = half
+    zt = LANES
     ahead = 3
     lead = 3
     z_steps = all_rows // zt
@@ -887,14 +887,16 @@
                 mean, inv, gamma, beta = stats(layer, v, cols)
 
                 def pieces():
-                    for b in BOTH:
-                        dx = mm(dbuf[at(2 * v + b, rows // 2)], wbuf[odd(n + 1)])
-                        for p in range(0, rows // 2, PIECE):
-                            some = pl.ds(b * (rows // 2) + p, PIECE)
+                    first = 0
+                    for size in (rows // 2, 3 * rows // 8, rows // 8):
+                        dx = mm(dbuf[pl.ds(pl.multiple_of(v * rows + first, LANES), size)], wbuf[odd(n + 1)])
+                        for p in range(0, size, PIECE):
+                            some = pl.ds(first + p, PIECE)
                             norm = (ubuf[slot, some] - mean) * inv
                             dy = jnp.where(norm * gamma + beta > 0, dx[p:p + PIECE], 0.0)
                             dyout[v, some] = dy
                             yield dy, dy * norm
+                        first += size
 
                 g = layer * items + i
                 acc[g] = two_sums(pieces())

time: 657 us -> 655 us (level)
  no operation moved by 1% of the time
where the time goes in v3:
time: 655 us; the launch traced here: 653 us
  Pallas kernels  652 us (100%)
    pallas_call x6, Pallas kernels, call(): pl.pallas_call(kernel, name=name, grid=grid, in_specs=in_specs, out_specs...  652 us

profile of v3, /device:TPU:0, one launch (start us, length us, event | category | flops | bytes accessed | tf_op | source)
XLA Modules:
  0.0 653.5 jit_solution(6484177277246058894)
XLA Ops:
  1.3 69.6 %fwd_first.1 = (f32[4096,2048]{1,0:T(8,128)}, f32[2,2,2048]{2,1,0:T(2,128)}, f32[2,2048]{1,0:T(2,128)}, f32[2,2048]{1,0:T(2,128)}, bf16[1024,2048]{1,0:T(8,128)(2,1)}, /*index=5*/bf16[2048,4096]{1,0:T(8,128)(2,1)}) custom-call(bf16[4096,2048]{1,0:T(8,128)(2,1)} %ha_ref.1, bf16[4096,2048]{1,0:T(8,128)(2,1)} %hb_ref.1, bf16[2048,1024]{1,0:T(8,128)(2,1)} %w_ref.1, ...), custom_call_target="tpu_custom_call" | custom-call | flops 34359738368 | bytes 100663296 | tf_op jit(solution)/shard_map/fwd_first/pallas_call | solution.py:215
  70.9 53.4 %fwd_next.2 = (bf16[2048,4096]{1,0:T(8,128)(2,1)}, f32[4096,2048]{1,0:T(8,128)}, f32[2,2,2048]{2,1,0:T(2,128)}, bf16[2048,2048]{1,0:T(8,128)(2,1)}, bf16[2048,1024]{1,0:T(8,128)(2,1)}) custom-call(f32[4096,2048]{1,0:T(8,128)} %get-tuple-element.39.u_ref.u1_ref, f32[2,2,2048]{2,1,0:T(2,128)} %get-tuple-element.40.s_ref.s1_ref, ...), custom_call_target="tpu_custom_call" | custom-call | flops 34359738368 | bytes 83886080 | tf_op jit(solution)/shard_map/fwd_next/pallas_call | solution.py:215
  124.3 50.0 %fwd_next.3 = (bf16[2048,4096]{1,0:T(8,128)(2,1)}, f32[4096,2048]{1,0:T(8,128)}, f32[2,2,2048]{2,1,0:T(2,128)}, bf16[2048,2048]{1,0:T(8,128)(2,1)}) custom-call(f32[4096,2048]{1,0:T(8,128)} %get-tuple-element.43.u_ref.u2_ref, f32[2,2,2048]{2,1,0:T(2,128)} %get-tuple-element.44.s_ref.s2_ref, f32[2,2048]{1,0:T(2,128)} %get-tuple-element.45.gb_ref.gb2_ref, ...), custom_call_target="tpu_custom_call" | custom-call | flops 34359738368 | bytes 83886080 | tf_op jit(solution)/shard_map/fwd_next/pallas_call | solution.py:215
  174.3 148.0 %corr_grad.1 = (bf16[2,2048,2048]{2,1,0:T(8,128)(2,1)}, f32[2,2048,2048]{2,1,0:T(8,128)}, f32[2,2,2048]{2,1,0:T(2,128)}, f32[1,128]{1,0:T(1,128)}) custom-call(f32[4096,2048]{1,0:T(8,128)} %get-tuple-element.47.z_ref, f32[2,2,2048]{2,1,0:T(2,128)} %get-tuple-element.48.s_ref.sz_ref, f32[1]{0:T(128)S(6)} %copy.18.lam_ref), custom_call_target="tpu_custom_call" | custom-call | flops 51539607552 | bytes 100663296 | tf_op jit(solution)/shard_map/corr_grad/pallas_call | solution.py:215
  322.3 315.0 %backward.1 = (f32[2048,1024]{1,0:T(8,128)}, f32[1024,2048]{1,0:T(8,128)}, f32[2048,1024]{1,0:T(8,128)}, f32[2,2,2,2048]{3,2,1,0:T(2,128)}, f32[4096,2048]{1,0:T...) custom-call(f32[4096,2048]{1,0:T(8,128)} %bitcast.19, ...), custom_call_target="tpu_custom_call" | custom-call | flops 171798691840 | bytes 335544320 | tf_op jit(solution)/shard_map/backward/pallas_call | solution.py:215
  637.3 16.2 %settle.1 = (f32[1,2048]{1,0:T(1,128)}, f32[1,2048]{1,0:T(1,128)}, f32[1,1024]{1,0:T(1,128)}, f32[1,1024]{1,0:T(1,128)}, f32[1,1]{1,0:T(1,128)}, /*index=5*/f32[...) custom-call(f32[2,2,2,2048]{3,2,1,0:T(2,128)} %get-tuple-element.57.sum_ref, ...), custom_call_target="tpu_custom_call" | custom-call | bytes 50331648 | tf_op jit(solution)/shard_map/settle/pallas_call | solution.py:215

commit v4 on v3

--- a/solution.py
+++ b/solution.py
@@ -542,6 +542,7 @@
                 for b in BOTH:
                     acc[1, :, at(b * n_chunk + t, width)] += sums[:, b * width:(b + 1) * width]
                     db_out(t, m, slot, b).start()
+                pl.when((t == n_chunk - 1) & (m == m_steps - 1))(lambda: share.start(1))
                 for cols in runs(dim, LANES):
                     da[at(m, mt), cols] += mm_bt(own, g[t, cols])
                 pl.when(t == n_chunk - 1)(lambda: finish(m))
@@ -586,7 +587,6 @@
                 pl.when(jnp.logical_and(t >= 0, t < n_chunk))(lambda t=t, stage_fn=stage_fn: stage_fn(t))
 
         loop(n_chunk + lead + 3, advance)
-        share.start(1)
         share.start(0)
         for t in range(n_chunk):
             for copy in (to_first(t), to_second(t), g_second(t, bit2), g_first(t, bit1), g_core(t, c)):
@@ -626,6 +626,7 @@
     per_layer = slabs * side
     n_chunk = n_layer * per_layer
     ahead = 3
+    n_mid = 4
     (u2, s2, gb2, w3_t, x1_t), (u1, s1, gb1, w2_t, h_t) = layers
 
     def kernel(d_ref, zh_ref, sz_ref, sd_ref, x2_ref, x1_ref, h_ref, u2_ref, u1_ref, w3_ref, w2_ref,
@@ -646,7 +647,7 @@
             return jnp.where(k == 0, 0, other(y))
 
         def m_slot(j):
-            return lax.rem(j, 4)
+            return lax.rem(j, n_mid)
 
         def copy(src, dst, sem):
             return pltpu.make_async_copy(src, dst, sem)
@@ -658,7 +659,7 @@
             return first + middle + last
 
         def begun(q):
-            return jnp.maximum(lax.div(q - 6, 2), 0)
+            return jnp.maximum(lax.div(q - 5, 2), 0)
 
         def to_core(s):
             return remote(psend.at[odd(s)], dr.at[odd(s)], ps.at[s], pr.at[s], cpeer)
@@ -745,7 +746,7 @@
         def end(j):
             load_part(j, 0).wait()
             load_part(j, 1).wait()
-            pl.when(j >= 4)(lambda: to_x(j).wait_send())
+            pl.when(j >= n_mid)(lambda: to_x(j).wait_send())
             mbuf[m_slot(j)] = ebuf[0] + ebuf[1]
             to_x(j).start()
             pl.when(j >= 2)(lambda: deliver(j - 2))
@@ -934,7 +935,8 @@
         ticks = (2 * n_layer - 1) * items
         chip_sum(n_slab - 1)
         issue(n_slab - 1, ticks)
-        ended = 36
+        ended = 37
+        end(ended - 1)
 
         def tail(j):
             begin(j, ticks + 2)
@@ -951,7 +953,7 @@
             remote(theirs, theirs, fcs.at[0], fcr.at[k], cpeer).wait_recv()
             sent = ry_ref.at[at(k, per_layer)]
             remote(sent, sent, ys.at[k], yr.at[0], ypeer).wait_send()
-        for j in range(n_chunk - 4, n_chunk):
+        for j in range(n_chunk - n_mid, n_chunk):
             to_x(j).wait_send()
 
     n_item = len(layers) * items
@@ -964,10 +966,10 @@
          sds((all_rows, dim), F32), sds((n_slab, half, width), F32), sds((n_chunk, piece, width), F32),
          sds((n_chunk, piece, width), F32)],
         [bf(all_rows, dim), bf(dim, all_rows), bf(2, dim, width), vm(2, rows, width), vm(2, rows, width), vm(2, rows, width),
-         vm(2, half, width), vm(2, half, width), vm(2, half, width), vm(3, piece, width), vm(4, piece, width),
+         vm(2, half, width), vm(2, half, width), vm(2, half, width), vm(3, piece, width), vm(n_mid, piece, width),
          vm(2, piece, width)] + Share.scratch(n_item, 2, width)
         + [TWO_DMA, TWO_DMA, TWO_DMA, TWO_DMA, TWO_DMA, DMA((n_slab,)), DMA((n_slab,)), DMA, DMA((n_layer,)),
-           DMA((n_chunk,)), DMA((4,)), DMA((n_chunk,)), DMA((3,)), TWO_DMA, TWO_DMA, DMA((n_layer,)),
+           DMA((n_chunk,)), DMA((n_mid,)), DMA((n_chunk,)), DMA((3,)), TWO_DMA, TWO_DMA, DMA((n_layer,)),
            pltpu.SemaphoreType.REGULAR],
         all_rows * dim * dim * 10, all_rows * dim * 40,
         (d_emb, zh, sz, s_emb, x2_t, x1_t, h_t, u2, u1, w3_t, w2_t, s2, s1, gb2, gb1))

time: 655 us -> 684 us (1.044)
  Pallas kernels: 652 us -> 681 us
    pallas_call x6, Pallas kernels: 652 us -> 681 us  [call(): pl.pallas_call(kernel, name=name, grid=grid, in_specs=in_specs, out_specs...]
where the time goes in v4:
time: 684 us; the launch traced here: 683 us
  Pallas kernels  681 us (100%)
    pallas_call x6, Pallas kernels, call(): pl.pallas_call(kernel, name=name, grid=grid, in_specs=in_specs, out_specs...  681 us

profile of v4, /device:TPU:0, one launch (start us, length us, event | category | flops | bytes accessed | tf_op | source)
XLA Modules:
  0.0 682.5 jit_solution(6887253651768595808)
XLA Ops:
  1.3 69.6 %fwd_first.1 = (f32[4096,2048]{1,0:T(8,128)}, f32[2,2,2048]{2,1,0:T(2,128)}, f32[2,2048]{1,0:T(2,128)}, f32[2,2048]{1,0:T(2,128)}, bf16[1024,2048]{1,0:T(8,128)(2,1)}, /*index=5*/bf16[2048,4096]{1,0:T(8,128)(2,1)}) custom-call(bf16[4096,2048]{1,0:T(8,128)(2,1)} %ha_ref.1, bf16[4096,2048]{1,0:T(8,128)(2,1)} %hb_ref.1, bf16[2048,1024]{1,0:T(8,128)(2,1)} %w_ref.1, ...), custom_call_target="tpu_custom_call" | custom-call | flops 34359738368 | bytes 100663296 | tf_op jit(solution)/shard_map/fwd_first/pallas_call | solution.py:215
  70.9 53.4 %fwd_next.2 = (bf16[2048,4096]{1,0:T(8,128)(2,1)}, f32[4096,2048]{1,0:T(8,128)}, f32[2,2,2048]{2,1,0:T(2,128)}, bf16[2048,2048]{1,0:T(8,128)(2,1)}, bf16[2048,1024]{1,0:T(8,128)(2,1)}) custom-call(f32[4096,2048]{1,0:T(8,128)} %get-tuple-element.39.u_ref.u1_ref, f32[2,2,2048]{2,1,0:T(2,128)} %get-tuple-element.40.s_ref.s1_ref, ...), custom_call_target="tpu_custom_call" | custom-call | flops 34359738368 | bytes 83886080 | tf_op jit(solution)/shard_map/fwd_next/pallas_call | solution.py:215
  124.3 50.0 %fwd_next.3 = (bf16[2048,4096]{1,0:T(8,128)(2,1)}, f32[4096,2048]{1,0:T(8,128)}, f32[2,2,2048]{2,1,0:T(2,128)}, bf16[2048,2048]{1,0:T(8,128)(2,1)}) custom-call(f32[4096,2048]{1,0:T(8,128)} %get-tuple-element.43.u_ref.u2_ref, f32[2,2,2048]{2,1,0:T(2,128)} %get-tuple-element.44.s_ref.s2_ref, f32[2,2048]{1,0:T(2,128)} %get-tuple-element.45.gb_ref.gb2_ref, ...), custom_call_target="tpu_custom_call" | custom-call | flops 34359738368 | bytes 83886080 | tf_op jit(solution)/shard_map/fwd_next/pallas_call | solution.py:215
  174.3 173.1 %corr_grad.1 = (bf16[2,2048,2048]{2,1,0:T(8,128)(2,1)}, f32[2,2048,2048]{2,1,0:T(8,128)}, f32[2,2,2048]{2,1,0:T(2,128)}, f32[1,128]{1,0:T(1,128)}) custom-call(f32[4096,2048]{1,0:T(8,128)} %get-tuple-element.47.z_ref, f32[2,2,2048]{2,1,0:T(2,128)} %get-tuple-element.48.s_ref.sz_ref, f32[1]{0:T(128)S(6)} %copy.18.lam_ref), custom_call_target="tpu_custom_call" | custom-call | flops 51539607552 | bytes 100663296 | tf_op jit(solution)/shard_map/corr_grad/pallas_call | solution.py:215
  347.4 318.8 %backward.1 = (f32[2048,1024]{1,0:T(8,128)}, f32[1024,2048]{1,0:T(8,128)}, f32[2048,1024]{1,0:T(8,128)}, f32[2,2,2,2048]{3,2,1,0:T(2,128)}, f32[4096,2048]{1,0:T...) custom-call(f32[4096,2048]{1,0:T(8,128)} %bitcast.19, ...), custom_call_target="tpu_custom_call" | custom-call | flops 171798691840 | bytes 335544320 | tf_op jit(solution)/shard_map/backward/pallas_call | solution.py:215
  666.3 16.2 %settle.1 = (f32[1,2048]{1,0:T(1,128)}, f32[1,2048]{1,0:T(1,128)}, f32[1,1024]{1,0:T(1,128)}, f32[1,1024]{1,0:T(1,128)}, f32[1,1]{1,0:T(1,128)}, /*index=5*/f32[...) custom-call(f32[2,2,2,2048]{3,2,1,0:T(2,128)} %get-tuple-element.57.sum_ref, ...), custom_call_target="tpu_custom_call" | custom-call | bytes 50331648 | tf_op jit(solution)/shard_map/settle/pallas_call | solution.py:215

commit v5 on v3

--- a/solution.py
+++ b/solution.py
@@ -380,9 +380,9 @@
         wtr_ref[...] = w[:, at(i, slab)].T
         v = i // steps
         keep = jnp.where(i % steps == 0, 0.0, 1.0)
-        for some in runs(dim, TM):
+        for some in runs(dim, half):
             o_ref[:, some] = mm(act[...], w[:, some])
-            for cols in runs(TM, LANES):
+            for cols in runs(half, LANES):
                 cols = pl.ds(some.start + cols.start, LANES)
                 share.acc[v, :, cols] = keep * share.acc[v, :, cols] + moments(o_ref, cols)
 

time: 655 us -> 655 us (level)
  no operation moved by 1% of the time
where the time goes in v5:
time: 655 us; the launch traced here: 653 us
  Pallas kernels  652 us (100%)
    pallas_call x6, Pallas kernels, call(): pl.pallas_call(kernel, name=name, grid=grid, in_specs=in_specs, out_specs...  652 us

profile of v5, /device:TPU:0, one launch (start us, length us, event | category | flops | bytes accessed | tf_op | source)
XLA Modules:
  0.0 653.5 jit_solution(6484177277246058894)
XLA Ops:
  1.3 69.6 %fwd_first.1 = (f32[4096,2048]{1,0:T(8,128)}, f32[2,2,2048]{2,1,0:T(2,128)}, f32[2,2048]{1,0:T(2,128)}, f32[2,2048]{1,0:T(2,128)}, bf16[1024,2048]{1,0:T(8,128)(2,1)}, /*index=5*/bf16[2048,4096]{1,0:T(8,128)(2,1)}) custom-call(bf16[4096,2048]{1,0:T(8,128)(2,1)} %ha_ref.1, bf16[4096,2048]{1,0:T(8,128)(2,1)} %hb_ref.1, bf16[2048,1024]{1,0:T(8,128)(2,1)} %w_ref.1, ...), custom_call_target="tpu_custom_call" | custom-call | flops 34359738368 | bytes 100663296 | tf_op jit(solution)/shard_map/fwd_first/pallas_call | solution.py:215
  70.9 53.4 %fwd_next.2 = (bf16[2048,4096]{1,0:T(8,128)(2,1)}, f32[4096,2048]{1,0:T(8,128)}, f32[2,2,2048]{2,1,0:T(2,128)}, bf16[2048,2048]{1,0:T(8,128)(2,1)}, bf16[2048,1024]{1,0:T(8,128)(2,1)}) custom-call(f32[4096,2048]{1,0:T(8,128)} %get-tuple-element.39.u_ref.u1_ref, f32[2,2,2048]{2,1,0:T(2,128)} %get-tuple-element.40.s_ref.s1_ref, ...), custom_call_target="tpu_custom_call" | custom-call | flops 34359738368 | bytes 83886080 | tf_op jit(solution)/shard_map/fwd_next/pallas_call | solution.py:215
  124.3 50.0 %fwd_next.3 = (bf16[2048,4096]{1,0:T(8,128)(2,1)}, f32[4096,2048]{1,0:T(8,128)}, f32[2,2,2048]{2,1,0:T(2,128)}, bf16[2048,2048]{1,0:T(8,128)(2,1)}) custom-call(f32[4096,2048]{1,0:T(8,128)} %get-tuple-element.43.u_ref.u2_ref, f32[2,2,2048]{2,1,0:T(2,128)} %get-tuple-element.44.s_ref.s2_ref, f32[2,2048]{1,0:T(2,128)} %get-tuple-element.45.gb_ref.gb2_ref, ...), custom_call_target="tpu_custom_call" | custom-call | flops 34359738368 | bytes 83886080 | tf_op jit(solution)/shard_map/fwd_next/pallas_call | solution.py:215
  174.3 148.0 %corr_grad.1 = (bf16[2,2048,2048]{2,1,0:T(8,128)(2,1)}, f32[2,2048,2048]{2,1,0:T(8,128)}, f32[2,2,2048]{2,1,0:T(2,128)}, f32[1,128]{1,0:T(1,128)}) custom-call(f32[4096,2048]{1,0:T(8,128)} %get-tuple-element.47.z_ref, f32[2,2,2048]{2,1,0:T(2,128)} %get-tuple-element.48.s_ref.sz_ref, f32[1]{0:T(128)S(6)} %copy.18.lam_ref), custom_call_target="tpu_custom_call" | custom-call | flops 51539607552 | bytes 100663296 | tf_op jit(solution)/shard_map/corr_grad/pallas_call | solution.py:215
  322.3 315.0 %backward.1 = (f32[2048,1024]{1,0:T(8,128)}, f32[1024,2048]{1,0:T(8,128)}, f32[2048,1024]{1,0:T(8,128)}, f32[2,2,2,2048]{3,2,1,0:T(2,128)}, f32[4096,2048]{1,0:T...) custom-call(f32[4096,2048]{1,0:T(8,128)} %bitcast.19, ...), custom_call_target="tpu_custom_call" | custom-call | flops 171798691840 | bytes 335544320 | tf_op jit(solution)/shard_map/backward/pallas_call | solution.py:215
  637.3 16.2 %settle.1 = (f32[1,2048]{1,0:T(1,128)}, f32[1,2048]{1,0:T(1,128)}, f32[1,1024]{1,0:T(1,128)}, f32[1,1024]{1,0:T(1,128)}, f32[1,1]{1,0:T(1,128)}, /*index=5*/f32[...) custom-call(f32[2,2,2,2048]{3,2,1,0:T(2,128)} %get-tuple-element.57.sum_ref, ...), custom_call_target="tpu_custom_call" | custom-call | bytes 50331648 | tf_op jit(solution)/shard_map/settle/pallas_call | solution.py:215
